TPU v7x, 32 devices: a whole 2x2x4 slice. The times are simulated.
32 devices in a mesh: ey: 8 (over z, y), ex: 4 (over x, core).
Axes of the slice: x: 2, y: 2, z: 4, core: 2. Of those that a mesh axis runs over, the one named last changes fastest.
Arguments:
- x: bfloat16 [512, 2048], P(('ey', 'ex'))
- kv_k: bfloat16 [512, 256, 4, 128], P(('ey', 'ex'))
- kv_v: bfloat16 [512, 256, 4, 128], P(('ey', 'ex'))
- lens: int32 [512], P(('ey', 'ex'))
- topk_idx: int32 [512, 8], P(('ey', 'ex'))
- gates: float32 [512, 8], P(('ey', 'ex'))
- ln1: bfloat16 [2048], replicated
- ln2: bfloat16 [2048], replicated
- wq: bfloat16 [2048, 4096], replicated
- wo: bfloat16 [4096, 2048], replicated
- ws1: bfloat16 [2048, 768], replicated
- ws3: bfloat16 [2048, 768], replicated
- ws2: bfloat16 [768, 2048], replicated
- w1: bfloat16 [128, 2048, 768], P(('ey', 'ex'))
- w3: bfloat16 [128, 2048, 768], P(('ey', 'ex'))
- w2: bfloat16 [128, 768, 2048], P(('ey', 'ex'))
Outputs:
- output: bfloat16 [512, 2048], P(('ey', 'ex'))
All inputs are finite; a program needn't handle non-finite values.
Results may differ from a plain program's by a relative error of at most 0.0121136.
Values are sent between devices in bfloat16 or wider.
A program may use at most 1 GiB of HBM per device.

v0:
```python
import jax
import jax.numpy as jnp
from jax import lax
from jax.sharding import PartitionSpec as P

EPS = 1e-6
BF = jnp.bfloat16
F32 = jnp.float32


def _rms(v, w):
    v = v.astype(F32)
    r = lax.rsqrt(jnp.mean(v * v, axis=-1, keepdims=True) + EPS)
    return (v * r * w.astype(F32)).astype(BF)


def _ffn(u, w1, w3, w2):
    g = jnp.dot(u, w1, preferred_element_type=F32)
    v = jnp.dot(u, w3, preferred_element_type=F32)
    z = (jax.nn.silu(g) * v).astype(BF)
    return jnp.dot(z, w2, preferred_element_type=F32).astype(BF)


def _experts(xin, w1, w3, w2):
    g = jnp.einsum('erd,edf->erf', xin, w1, preferred_element_type=F32)
    v = jnp.einsum('erd,edf->erf', xin, w3, preferred_element_type=F32)
    z = (jax.nn.silu(g) * v).astype(BF)
    return jnp.einsum('erf,efd->erd', z, w2, preferred_element_type=F32).astype(BF)


def _attn(x, kk, vv, lens, ln1, wq, wo):
    b, l, kvh, dh = kk.shape
    hq = wq.shape[1] // dh
    a = _rms(x, ln1)
    q = jnp.dot(a, wq, preferred_element_type=F32).astype(BF).reshape(b, kvh, hq // kvh, dh)
    s = jnp.einsum('bkgd,blkd->bkgl', q, kk, preferred_element_type=F32) * dh ** -0.5
    valid = jnp.arange(l)[None, :] < lens[:, None]
    s = jnp.where(valid[:, None, None, :], s, -jnp.inf)
    p = jax.nn.softmax(s, axis=-1).astype(BF)
    o = jnp.einsum('bkgl,blkd->bkgd', p, vv, preferred_element_type=F32).astype(BF)
    attn = jnp.dot(o.reshape(b, hq * dh), wo, preferred_element_type=F32)
    return (x.astype(F32) + attn).astype(BF)


def _ranks(topk, n_exp):
    chosen = (topk[..., None] == jnp.arange(n_exp)).any(axis=-2).astype(jnp.int32)
    before = jnp.cumsum(chosen, axis=-2) - chosen
    return jnp.take_along_axis(before, topk, axis=-1)


def solution(mesh):
    ey, ex = mesh.shape['ey'], mesh.shape['ex']
    ndev = ey * ex
    rows = P(('ey', 'ex'))
    rep = P()

    def local(x, kv_k, kv_v, lens, topk_idx, gates, ln1, ln2, wq, wo, ws1, ws3, ws2, w1, w3, w2):
        b, d = x.shape
        k = topk_idx.shape[1]
        edev = w1.shape[0]
        n_exp = edev * ndev
        cap = max(4, (2 * b * k + n_exp - 1) // n_exp)
        nslotv = ex * edev * ey * cap
        iy = lax.axis_index('ey')

        h = _attn(x, kv_k, kv_v, lens, ln1, wq, wo)
        u = _rms(h, ln2)

        u_g = lax.all_gather(u, 'ey')
        t_g = lax.all_gather(topk_idx, 'ey')
        g_g = lax.all_gather(gates, 'ey')

        rank = _ranks(t_g, n_exp)
        mine = (t_g // (edev * ex) == iy) & (rank < cap)
        src = jnp.arange(ey, dtype=jnp.int32)[:, None, None]
        dest = ((t_g // edev) % ex) * edev + t_g % edev
        pos = jnp.where(mine, (dest * ey + src) * cap + rank, nslotv).reshape(-1)
        tok = jnp.broadcast_to(jnp.arange(ey * b, dtype=jnp.int32).reshape(ey, b, 1), t_g.shape).reshape(-1)
        slot_tok = jnp.full((nslotv,), ey * b, jnp.int32).at[pos].set(tok, mode='drop')
        slot_gate = jnp.zeros((nslotv,), F32).at[pos].set(g_g.reshape(-1), mode='drop')
        u_pad = jnp.concatenate([u_g.reshape(ey * b, d), jnp.zeros((1, d), BF)], axis=0)

        send = u_pad[slot_tok].reshape(ex, edev, ey * cap, d)
        recv = lax.all_to_all(send, 'ex', 0, 0)
        xin = recv.transpose(1, 0, 2, 3).reshape(edev, ex * ey * cap, d)
        out = _experts(xin, w1, w3, w2)
        back = out.reshape(edev, ex, ey * cap, d).transpose(1, 0, 2, 3)
        ret = lax.all_to_all(back, 'ex', 0, 0).reshape(nslotv, d)

        partial = jnp.zeros((ey * b + 1, d), F32).at[slot_tok].add(slot_gate[:, None] * ret.astype(F32))
        routed = lax.psum_scatter(partial[: ey * b].reshape(ey, b, d), 'ey', scatter_dimension=0)
        y = h.astype(F32) + _ffn(u, ws1, ws3, ws2).astype(F32) + routed
        return y.astype(BF)

    return jax.shard_map(
        local, mesh=mesh,
        in_specs=(rows, rows, rows, rows, rows, rows, rep, rep, rep, rep, rep, rep, rep, rows, rows, rows),
        out_specs=rows, check_vma=False)
```

profile of v0, /device:TPU:0, one launch (start us, length us, event | category | flops | bytes accessed | tf_op | source)
XLA Modules:
  0.0 300.5 jit_solution(5201737600758303651)
XLA Ops:
  6.5 32.4 %all-gather.3 = s32[8,16,8]{1,2,0:T(8,128)S(1)} all-gather(s32[1,16,8]{1,2,0:T(8,128)} %bitcast.63), channel_id=2, replica_groups=mesh['ey'=8,'ex'=4] {'ey'}, dimensions={0}, use_global_device_ids=true | all-gather | bytes 4608 | tf_op jit(solution)/shard_map/all_gather | solution.py:70
  40.6 1.0 fusion.29
  41.6 8.1 %fusion.24 = bf16[2,8,32,128]{3,1,2,0:T(8,128)(2,1)S(1)} fusion(bf16[2048,4096]{1,0:T(8,128)(2,1)} %param.24, bf16[16,2048]{1,0:T(8,128)(2,1)} %param.16, f32[2048]{0:T(1024)S(1)} %convert_element_type.60, f32[16]{0:T(128)S(1)} %add_rsqrt_fusion.1), kind=kOutput, calls=%fused_computation.30 | convolution fusion | flops 268632064 | bytes 16982080 | tf_op jit(solution)/shard_map/dot_general | solution.py:35
  49.9 4.3 %fusion.63 = (f32[16,4,8]{2,1,0:T(4,128)S(1)}, f32[16,4,8,256]{3,2,1,0:T(8,128)}) fusion(bf16[16,4,8,128]{3,2,1,0:T(8,128)(2,1)S(1)} %bitcast.62, bf16[16,256,4,128]{3,2,1,0:T(4,128)(2,1)} %param.17, pred[16,256]{1,0:T(8,128)(4,1)S(1)} %iota_compare_fusion.1), kind=kOutput, calls=%fused_computation.97 | convolution fusion | flops 34078976 | bytes 4855808 | tf_op jit(solution)/shard_map/sub | solution.py:39
  54.1 3.1 %fusion.21 = bf16[16,4,8,128]{3,2,1,0:T(8,128)(2,1)S(1)} fusion(bf16[16,256,4,128]{3,2,1,0:T(4,128)(2,1)} %param.18, f32[16,4,8,256]{3,2,1,0:T(8,128)} %get-tuple-element.6, f32[16,4,8]{2,1,0:T(4,128)S(1)} %get-tuple-element.5), kind=kOutput, calls=%fused_computation.29 | convolution fusion | flops 33882112 | bytes 4851712 | tf_op jit(solution)/shard_map/bkgl,blkd->bkgd/dot_general | solution.py:40
  57.3 8.2 %multiply_reduce_fusion = (f32[16]{0:T(128)S(1)}, f32[16,2048]{1,0:T(8,128)S(1)}) fusion(bf16[4096,2048]{1,0:T(8,128)(2,1)} %param.25, bf16[2,8,32,128]{3,2,1,0:T(8,128)(2,1)S(1)} %bitcast.61, bf16[16,2048]{1,0:T(8,128)(2,1)S(1)} %copy-done.2), kind=kOutput, calls=%fused_computation.47 | convolution fusion | flops 268632064 | bytes 17104960 | tf_op jit(solution)/shard_map/dot_general | solution.py:41
  65.6 31.2 %all-gather.2 = bf16[128,2048]{1,0:T(8,128)(2,1)} all-gather(bf16[16,2048]{1,0:T(8,128)(2,1)S(1)} %multiply_convert_fusion.1), channel_id=4, replica_groups=mesh['ey'=8,'ex'=4] {'ey'}, dimensions={0}, use_global_device_ids=true | all-gather | bytes 589824 | tf_op jit(solution)/shard_map/all_gather | solution.py:69
  96.9 6.5 %gather_fusion.1 = s32[1024]{0:T(1024)S(1)} fusion(s32[8,16,128]{2,0,1:T(8,128)S(1)} %reduce-window_subtract_fusion, s32[1024]{0:T(1024)S(1)} %reshape.149), kind=kCustom, calls=%fused_computation.1 | custom fusion | bytes 20480 | tf_op jit(solution)/shard_map/jit(take_along_axis)/gather | solution.py:48
  103.9 4.3 %scatter_custom_fusion = s32[512]{0:T(512)S(1)} fusion(s32[1024]{0:T(1024)S(1)} %bitcast.65, s32[1024]{0:T(1024)S(1)} %reshape.159, s32[]{:T(128)} %constant.86.clone.1), kind=kCustom, calls=%fused_computation.92 | custom fusion | bytes 2052 | tf_op jit(solution)/shard_map/scatter | solution.py:79
  108.2 1.9 concatenate.3
  110.1 6.4 %gather_fusion = bf16[512,2048]{1,0:T(8,128)(2,1)} fusion(bf16[129,2048]{1,0:T(8,128)(2,1)} %concatenate.3, s32[1024]{0:T(1024)S(1)} %pad_clamp_fusion), kind=kCustom, calls=%fused_computation | custom fusion | bytes 4196352 | tf_op jit(solution)/shard_map/gather | solution.py:83
  116.6 29.0 %all_to_all.10 = bf16[4,4,32,2048]{3,2,1,0:T(8,128)(2,1)S(1)} all-to-all(bf16[4,4,32,2048]{3,2,1,0:T(8,128)(2,1)} %bitcast.54), channel_id=1, replica_groups=mesh['ey'=8,'ex'=4] {'ex'}, dimensions={0} | all-to-all | bytes 4194304 | tf_op jit(solution)/shard_map/all_to_all | solution.py:84
  145.7 1.3 copy-done.1
  147.0 7.6 %fusion.67 = f32[4,128,768]{2,1,0:T(8,128)} fusion(bf16[4,128,2048]{2,1,0:T(8,128)(2,1)S(1)} %bitcast.57, bf16[4,2048,768]{2,1,0:T(8,128)(2,1)} %param.29), kind=kOutput, calls=%fused_computation.99 | convolution fusion | flops 1610612736 | bytes 16252928 | tf_op jit(solution)/shard_map/erd,edf->erf/dot_general | solution.py:25
  154.6 14.4 %convolution_convert_fusion.1 = bf16[4,128,2048]{2,1,0:T(8,128)(2,1)} fusion(bf16[4,768,2048]{2,1,0:T(8,128)(2,1)} %param.31, f32[4,128,768]{2,1,0:T(8,128)} %fusion.67, bf16[4,128,2048]{2,1,0:T(8,128)(2,1)} %bitcast.58, bf16[4,2048,768]{2,1,0:T(8,128)(2,1)} %param.30), kind=kOutput, calls=%fused_computation.13 | convolution fusion | flops 3224633344 | bytes 30932992 | tf_op jit(solution)/shard_map/erf,efd->erd/dot_general | solution.py:28
  169.0 3.1 %copy.81 = bf16[4,4,32,2048]{3,2,0,1:T(8,128)(2,1)} copy(bf16[4,4,32,2048]{3,2,1,0:T(8,128)(2,1)} %bitcast.60) | data formatting | bytes 4194304 | tf_op jit(solution)/shard_map/reshape | solution.py:87
  172.1 4.6 %all-to-all-start.1 = ((bf16[4,4,32,2048]{3,2,1,0:T(8,128)(2,1)}), bf16[4,4,32,2048]{3,2,1,0:T(8,128)(2,1)}, u32[]{:S(2)}, u32[]{:S(2)}) async-start(bf16[4,4,32,2048]{3,2,1,0:T(8,128)(2,1)} %bitcast.55), calls=%async_computation.1 | async-start | bytes 4194304 | tf_op jit(solution)/shard_map/all_to_all | solution.py:88
  176.8 30.4 %all-gather.4 = f32[8,16,8]{1,2,0:T(8,128)S(1)} all-gather(f32[1,16,8]{1,2,0:T(8,128)S(1)} %bitcast.64), channel_id=3, replica_groups=mesh['ey'=8,'ex'=4] {'ey'}, dimensions={0}, use_global_device_ids=true | all-gather | bytes 4608 | tf_op jit(solution)/shard_map/all_gather | solution.py:71
  207.4 4.5 %scatter_custom_fusion.1 = f32[512]{0:T(512)S(1)} fusion(s32[1024]{0:T(1024)S(1)} %bitcast.66, f32[1024]{0:T(1024)S(1)} %reshape.167, f32[]{:T(128)} %constant.80.clone.1), kind=kCustom, calls=%fused_computation.90 | custom fusion | bytes 2052 | tf_op jit(solution)/shard_map/scatter | solution.py:80
  211.9 9.2 %scatter_custom_fusion.2 = f32[129,2048]{1,0:T(8,128)} fusion(s32[512]{0:T(512)S(1)} %compare_select_fusion.1, bf16[512,2048]{1,0:T(8,128)(2,1)} %bitcast.12, f32[512]{0:T(512)S(1)} %scatter_custom_fusion.1, f32[]{:T(128)} %constant.80.clone.1), kind=kCustom, calls=%fused_computation.8 | custom fusion | flops 3145728 | bytes 3155972 | tf_op jit(solution)/shard_map/scatter-add | solution.py:90
  221.2 2.3 slice.9
  223.5 2.4 fusion.66
  225.9 64.1 %reduce-scatter.2.cloned.1.call-done = f32[1,16,2048]{2,1,0:T(8,128)} async-done(((f32[8,16,2048]{2,1,0:T(8,128)}), f32[1,16,2048]{2,1,0:T(8,128)}) %reduce-scatter.2.cloned.1.call-update) | async-done | bytes 131088 | tf_op jit(solution)/shard_map/reduce_scatter | solution.py:91
  290.0 3.7 %fusion.9 = bf16[16,2048]{1,0:T(8,128)(2,1)} fusion(f32[16,2048]{1,0:T(8,128)S(1)} %get-tuple-element.8, bf16[768,2048]{1,0:T(8,128)(2,1)S(1)} %copy-done, bf16[16,2048]{1,0:T(8,128)(2,1)S(1)} %multiply_convert_fusion.1, bf16[2048,768]{1,0:T(8,128)(2,1)} %param.27, f32[1,16,2048]{2,1,0:T(8,128)} %reduce-scatter.2.cloned.1.call-done, f32[16,768]{1,0:T(8,128)S(1)} %fusion.66), kind=kOutput, calls=%fused_computation.19 | convolution fusion | flops 100900864 | bytes 6733824 | tf_op jit(solution)/shard_map/dot_general | solution.py:21
  (40 shorter events, 2.9 us)
Async XLA Ops:
  6.5 283.5 %copy-start = (bf16[768,2048]{1,0:T(8,128)(2,1)S(1)}, bf16[768,2048]{1,0:T(8,128)(2,1)}, u32[]{:S(2)}) copy-start(bf16[768,2048]{1,0:T(8,128)(2,1)} %param.28) | copy-start | bytes 9437188
  41.6 8.2 %copy-start.6 = (s32[16]{0:T(128)S(1)}, s32[16]{0:T(128)}, u32[]{:S(2)}) copy-start(s32[16]{0:T(128)} %param.19) | copy-start | bytes 196
  54.1 3.1 %copy-start.2 = (bf16[16,2048]{1,0:T(8,128)(2,1)S(1)}, bf16[16,2048]{1,0:T(8,128)(2,1)}, u32[]{:S(2)}) copy-start(bf16[16,2048]{1,0:T(8,128)(2,1)} %param.16) | copy-start | bytes 196612
  57.2 8.2 %copy-start.4 = (bf16[2048]{0:T(1024)(128)(2,1)S(1)}, bf16[2048]{0:T(1024)(128)(2,1)}, u32[]{:S(2)}) copy-start(bf16[2048]{0:T(1024)(128)(2,1)} %param.23) | copy-start | bytes 12292
  57.2 39.5 %copy-start.3 = (pred[8,16,128]{2,1,0:T(8,128)(4,1)S(1)}, pred[8,16,128]{2,1,0:T(8,128)(4,1)}, u32[]{:S(2)}) copy-start(pred[8,16,128]{2,1,0:T(8,128)(4,1)} %fusion.27) | copy-start | bytes 49156
  145.7 1.3 copy-start.1
  172.1 4.6 %copy-start.5 = (f32[16,8]{0,1:T(8,128)S(1)}, f32[16,8]{0,1:T(8,128)}, u32[]{:S(2)}) copy-start(f32[16,8]{0,1:T(8,128)} %param.21) | copy-start | bytes 1540
  172.1 39.8 %all-to-all-start.1 = ((bf16[4,4,32,2048]{3,2,1,0:T(8,128)(2,1)}), bf16[4,4,32,2048]{3,2,1,0:T(8,128)(2,1)}, u32[]{:S(2)}, u32[]{:S(2)}) async-start(bf16[4,4,32,2048]{3,2,1,0:T(8,128)(2,1)} %bitcast.55), calls=%async_computation.1 | async-start | bytes 4194304 | tf_op jit(solution)/shard_map/all_to_all | solution.py:88
  176.7 113.3 %reduce-scatter.2.cloned.1.call-start = ((), (), s32[]{:S(2)}) async-start(), calls=%async_computation.3 | async-start | bytes 1179648 | tf_op jit(solution)/shard_map/reduce_scatter | solution.py:91
Sparse Core Ops, SparseCore 0:
  223.6 66.3 reduce-scatter.1
where the time goes:
time: 301 us
  blocking collectives  123 us (41%)
  waiting for transfers between devices  64.1 us (21%)
  matrix products  51.8 us (17%)
  local copies, waits for them, and re-layouts  31.2 us (10%)
  between operations  13.6 us (5%)
  other arithmetic  12.1 us (4%)
  starting transfers between devices  4.61 us (2%)
    reduce_scatter x1, waiting for transfers between devices, local(): lax.psum_scatter(partial[:ey * b].reshape(ey, b, d), 'ey', scatter_dimens...  64.1 us
    all_gather x1, blocking collectives, local(): t_g = lax.all_gather(topk_idx, 'ey')  32.4 us
    all_gather x1, blocking collectives, local(): u_g = lax.all_gather(u, 'ey')  31.2 us
    all_gather x1, blocking collectives, local(): g_g = lax.all_gather(gates, 'ey')  30.4 us
    all_to_all x1, blocking collectives, local(): recv = lax.all_to_all(send, 'ex', 0, 0)  29 us
    dot_general x1, matrix products, _experts(): jnp.einsum('erf,efd->erd', z, w2, preferred_element_type=F32).astype(BF)  14.4 us
    scatter-add x1, other arithmetic, local(): jnp.zeros((ey * b + 1, d), F32).at[slot_tok]  9.23 us
    dot_general x1, matrix products, _attn(): attn = jnp.dot(o.reshape(b, hq * dh), wo, preferred_element_type=F32)  8.19 us
  transfers between devices with their start and end apart: 2, of which 1 were waited for; matrix products, arithmetic and copies ran while one was open for 2% of the time, Pallas kernels for 0%

commit v1 on v0

v1 whole, which is shorter than its diff:
```python
import functools

import jax
import jax.numpy as jnp
from jax import lax
from jax.experimental import pallas as pl
from jax.experimental.pallas import tpu as pltpu
from jax.sharding import PartitionSpec as P

EPS = 1e-6
BF = jnp.bfloat16
F32 = jnp.float32
I32 = jnp.int32

D = 2048
FF = 768
NT = 512
CAPE = 4
NC = 4
CW = D // NC
MW = 128


def _rms(v, w):
    v = v.astype(F32)
    r = lax.rsqrt(jnp.mean(v * v, axis=-1, keepdims=True) + EPS)
    return (v * r * w.astype(F32)).astype(BF)


def _attn(x, kk, vv, lens, ln1, wq, wo):
    b, l, kvh, dh = kk.shape
    hq = wq.shape[1] // dh
    a = _rms(x, ln1)
    q = jnp.dot(a, wq, preferred_element_type=F32).astype(BF).reshape(b, kvh, hq // kvh, dh)
    s = jnp.einsum('bkgd,blkd->bkgl', q, kk, preferred_element_type=F32) * dh ** -0.5
    valid = jnp.arange(l)[None, :] < lens[:, None]
    s = jnp.where(valid[:, None, None, :], s, -jnp.inf)
    p = jax.nn.softmax(s, axis=-1).astype(BF)
    o = jnp.einsum('bkgl,blkd->bkgd', p, vv, preferred_element_type=F32).astype(BF)
    attn = jnp.dot(o.reshape(b, hq * dh), wo, preferred_element_type=F32)
    return (x.astype(F32) + attn).astype(BF)


def _split3(v):
    a = v.astype(BF)
    r = v - a.astype(F32)
    b = r.astype(BF)
    c = (r - b.astype(F32)).astype(BF)
    return a, b, c


def _dot(a, b):
    return jnp.dot(a, b, preferred_element_type=F32)


def _dot_tt(a, b):
    return lax.dot_general(a, b, (((1,), (1,)), ((), ())), preferred_element_type=F32)


def _dot_00(a, b):
    return lax.dot_general(a, b, (((0,), (0,)), ((), ())), preferred_element_type=F32)


def _moe_kernel(cap, ue_ref, h_ref, ws1, ws3, ws2, w1, w3, w2, out_ref,
                u0, u1, u2, u3, wa, wb, wc, xe, zz, fc, gm, lmat,
                ps, ra, rx, ry, dz_buf, rz, base,
                wsem, ags, agr, cbs, cbr):
    us = (u0, u1, u2, u3)
    iy = lax.axis_index('ey')
    ix = lax.axis_index('ex')
    z, y = iy // 2, iy % 2
    x, k = ix // 2, ix % 2
    dev = iy * 4 + ix

    def zdev(d):
        return (((z + d) % 4) * 2 + y, ix)
    ydev = (z * 2 + (1 - y), ix)
    xdev = (iy, (1 - x) * 2 + k)
    kdev = (iy, x * 2 + (1 - k))

    barrier = pltpu.get_barrier_semaphore()
    for d in (zdev(1), zdev(2), zdev(3), ydev, xdev, kdev):
        pl.semaphore_signal(barrier, inc=1, device_id=d, device_id_type=pl.DeviceIdType.MESH)

    def wcopies(slot, a, b, c, i):
        return [pltpu.make_async_copy(a, wa.at[slot], wsem.at[i, 0]),
                pltpu.make_async_copy(b, wb.at[slot], wsem.at[i, 1]),
                pltpu.make_async_copy(c, wc.at[slot], wsem.at[i, 2])]
    shared_cp = wcopies(0, ws1, ws3, ws2, 4)
    exp_cp = [wcopies((e + 1) % 4, w1.at[e], w3.at[e], w2.at[e], e) for e in range(4)]
    for cp in shared_cp:
        cp.start()
    for e in range(3):
        for cp in exp_cp[e]:
            cp.start()

    pl.semaphore_wait(barrier, 6)

    def rcopy(src, dst, s, r, d):
        return pltpu.make_async_remote_copy(src_ref=src, dst_ref=dst, send_sem=s, recv_sem=r,
                                            device_id=d, device_id_type=pl.DeviceIdType.MESH)

    offs = [0] + [MW + CW * c for c in range(1, NC)]
    wid = [MW + CW] + [CW] * (NC - 1)
    zc = []
    for c in range(NC):
        src = ue_ref.at[:, pl.ds(offs[c], wid[c])]
        cps = [rcopy(src, us[c].at[z, y, x, k], ags.at[c, d - 1], agr.at[c, d - 1], zdev(d)) for d in (1, 2, 3)]
        for cp in cps:
            cp.start()
        zc.append(cps)
        us[c][z, y, x, k] = ue_ref[:, offs[c]:offs[c] + wid[c]]

    for cp in shared_cp[:2]:
        cp.wait()
    u = ue_ref[:, MW:]
    g = _dot(u, wa[0])
    v = _dot(u, wb[0])
    zs = (jax.nn.silu(g) * v).astype(BF)
    shared_cp[2].wait()
    base[...] = h_ref[...].astype(F32) + _dot(zs, wc[0]).astype(BF).astype(F32)
    for cp in exp_cp[3]:
        cp.start()

    p1 = []
    for c in range(NC):
        for cp in zc[c]:
            cp.wait_recv()
        blk = us[c].at[:, y, x, k]
        cp = rcopy(blk, blk, ags.at[c, 3], agr.at[c, 3], ydev if c % 2 == 0 else xdev)
        cp.start()
        p1.append(cp)
    p2 = []
    for c in range(NC):
        p1[c].wait_recv()
        blk = us[c].at[:, :, x, k] if c % 2 == 0 else us[c].at[:, y, :, k]
        cp = rcopy(blk, blk, ags.at[c, 4], agr.at[c, 4], xdev if c % 2 == 0 else ydev)
        cp.start()
        p2.append(cp)
    p3 = []
    for c in range(NC):
        p2[c].wait_recv()
        blk = us[c].at[:, :, :, k]
        cp = rcopy(blk, blk, ags.at[c, 5], agr.at[c, 5], kdev)
        cp.start()
        p3.append(cp)
    p3[0].wait_recv()

    mt = u0[...].reshape(NT, MW + CW)[:, :MW].astype(F32).T
    tk = mt[0:8]
    gts = (mt[8:16], mt[16:24], mt[24:32])
    t1 = lax.broadcasted_iota(I32, (1, NT), 1)
    blk1 = t1 // 16
    ti = lax.broadcasted_iota(I32, (NT, NT), 0)
    tj = lax.broadcasted_iota(I32, (NT, NT), 1)
    earlier = ti < tj
    lmat[...] = jnp.where(earlier & (ti // 16 == tj // 16), 1.0, 0.0).astype(BF)
    ms, gs = [], []
    for e in range(4):
        eq = tk == (dev * 4 + e).astype(F32)
        ms.append(jnp.sum(jnp.where(eq, 1.0, 0.0), axis=0, keepdims=True))
        gs.append([jnp.sum(jnp.where(eq, gg, 0.0), axis=0, keepdims=True) for gg in gts])
    mstack = jnp.concatenate(ms + [jnp.zeros((4, NT), F32)], axis=0)
    before = _dot(mstack.astype(BF), lmat[...])
    slot = jnp.where((mstack > 0.5) & (before < CAPE - 0.5), (blk1 * CAPE).astype(F32) + before, -1.0)

    lmat[...] = jnp.where(earlier & ((ti // 16) % 8 == (tj // 16) % 8), 1.0, 0.0).astype(BF)

    def rowmatch(r):
        lo = (r * 16).astype(F32)
        return jnp.max(jnp.where((tk >= lo) & (tk < lo + 16.0), 1.0, 0.0), axis=0, keepdims=True)
    rm = jnp.concatenate([rowmatch(iy), rowmatch(z * 2 + (1 - y)), jnp.zeros((6, NT), F32)], axis=0)
    rb = _dot(rm.astype(BF), lmat[...])
    ridx = jnp.where((rm > 0.5) & (rb < cap - 0.5), rb, -1.0)
    gidx = ((blk1 % 2) * 2 + (blk1 // 2) % 2) * 2 + (blk1 // 4) % 2
    cidx = jnp.where(ridx[0:1] > -0.5, (gidx * cap).astype(F32) + ridx[0:1], -1.0)
    cmat = (lax.broadcasted_iota(I32, (8 * cap, NT), 0).astype(F32) == cidx).astype(F32).astype(BF)
    mine = gidx == (k * 2 + x) * 2 + y
    ci = lax.broadcasted_iota(I32, (cap, NT), 0).astype(F32)
    own = jnp.concatenate([(ci == jnp.where(mine, ridx[0:1], -1.0)).astype(F32),
                           (ci == jnp.where(mine, ridx[1:2], -1.0)).astype(F32)], axis=0).astype(BF)
    sj = lax.broadcasted_iota(I32, (NT, 64), 1)
    st = lax.broadcasted_iota(I32, (NT, 64), 0)
    sel = (st == (sj // 16) * 128 + y * 64 + ix * 16 + sj % 16).astype(F32).astype(BF)
    emat = _dot(own, sel).astype(BF)

    si = lax.broadcasted_iota(I32, (128, NT), 0).astype(F32)
    for e in range(4):
        hit = si == slot[e:e + 1]
        pe = hit.astype(F32).astype(BF)
        for m in range(3):
            gp = jnp.where(hit, gs[e][m], 0.0).astype(BF)
            gm[m, :, 128 * e:128 * (e + 1)] = _dot_tt(cmat, gp).astype(BF)
        xe[e, :, :NT] = pe

    for c in range(1, NC):
        p3[c].wait_recv()
    for e in range(4):
        pe = xe[e, :, :NT]
        for c in range(NC):
            off = MW if c == 0 else 0
            uc = us[c][...].reshape(NT, wid[c])[:, off:]
            fc[0:128, :] = _dot(pe, uc).astype(BF)
            if c > 0:
                xe[e, :, c * CW:(c + 1) * CW] = fc[0:128, :]
            else:
                fc[128:256, :] = fc[0:128, :]
        xe[e, :, :CW] = fc[128:256, :]
    for e in range(4):
        s_ = (e + 1) % 4
        exp_cp[e][0].wait()
        g = _dot(xe[e], wa[s_])
        exp_cp[e][1].wait()
        v = _dot(xe[e], wb[s_])
        zz[e] = (jax.nn.silu(g) * v).astype(BF)
    for e in range(4):
        exp_cp[e][2].wait()

    sent = []
    ca, cx, cy, cz = {}, {}, {}, {}

    def stage0(c):
        for e in range(4):
            fc[128 * e:128 * (e + 1), :] = _dot(zz[e], wc[(e + 1) % 4, :, c * CW:(c + 1) * CW]).astype(BF)
        f = fc[...]
        o = _dot(gm[0], f) + _dot(gm[1], f) + _dot(gm[2], f)
        ps[c] = o.reshape(2, 2, 2, cap, CW)
        cp = rcopy(ps.at[c, 1 - k], ra.at[c], cbs.at[c, 0], cbr.at[c, 0], kdev)
        cp.start()
        ca[c] = cp

    def stage1(c):
        ca[c].wait_recv()
        ps[c, k] = ps[c, k] + ra[c]
        cp = rcopy(ps.at[c, k, 1 - x], rx.at[c], cbs.at[c, 1], cbr.at[c, 1], xdev)
        cp.start()
        cx[c] = cp

    def stage2(c):
        cx[c].wait_recv()
        ps[c, k, x] = ps[c, k, x] + rx[c]
        cp = rcopy(ps.at[c, k, x, 1 - y], ry.at[c], cbs.at[c, 2], cbr.at[c, 2], ydev)
        cp.start()
        cy[c] = cp

    def stage3(c):
        cy[c].wait_recv()
        data = jnp.concatenate([ps[c, k, x, y], ry[c]], axis=0)
        a, b, d = _split3(data)
        dn = _dot_00(emat, a) + _dot_00(emat, b) + _dot_00(emat, d)
        dz_buf[c] = dn.reshape(4, 16, CW)
        cps = [rcopy(dz_buf.at[c, (z + d) % 4], rz.at[c, d - 1], cbs.at[c, 2 + d], cbr.at[c, 2 + d], zdev(d)) for d in (1, 2, 3)]
        for cp in cps:
            cp.start()
        cz[c] = cps

    def stage4(c):
        for cp in cz[c]:
            cp.wait_recv()
        o = base[:, c * CW:(c + 1) * CW] + dz_buf[c, z] + rz[c, 0] + rz[c, 1] + rz[c, 2]
        out_ref[:, c * CW:(c + 1) * CW] = o.astype(BF)

    stages = (stage0, stage1, stage2, stage3, stage4)
    for step in range(NC + 4):
        for s_, fn in enumerate(stages):
            c = step - s_
            if 0 <= c < NC:
                fn(c)
    for c in range(NC):
        for cp in zc[c] + [p1[c], p2[c], p3[c], ca[c], cx[c], cy[c]] + cz[c]:
            cp.wait_send()


def _moe(cap, cid, ue, h, ws1, ws3, ws2, w1, w3, w2):
    vm = pl.BlockSpec(memory_space=pltpu.VMEM)
    hb = pl.BlockSpec(memory_space=pl.ANY)
    widths = [MW + CW] + [CW] * (NC - 1)
    scratch = [pltpu.VMEM((4, 2, 2, 2, 16, w), BF) for w in widths] + [
        pltpu.VMEM((4, D, FF), BF), pltpu.VMEM((4, D, FF), BF), pltpu.VMEM((4, FF, D), BF),
        pltpu.VMEM((4, 128, D), BF), pltpu.VMEM((4, 128, FF), BF), pltpu.VMEM((512, CW), BF),
        pltpu.VMEM((3, 8 * cap, 512), BF), pltpu.VMEM((NT, NT), BF),
        pltpu.VMEM((NC, 2, 2, 2, cap, CW), F32), pltpu.VMEM((NC, 2, 2, cap, CW), F32),
        pltpu.VMEM((NC, 2, cap, CW), F32), pltpu.VMEM((NC, cap, CW), F32),
        pltpu.VMEM((NC, 4, 16, CW), F32), pltpu.VMEM((NC, 3, 16, CW), F32),
        pltpu.VMEM((16, D), F32),
        pltpu.SemaphoreType.DMA((5, 3)), pltpu.SemaphoreType.DMA((NC, 6)), pltpu.SemaphoreType.DMA((NC, 6)),
        pltpu.SemaphoreType.DMA((NC, 6)), pltpu.SemaphoreType.DMA((NC, 6)),
    ]
    return pl.pallas_call(
        functools.partial(_moe_kernel, cap),
        out_shape=jax.ShapeDtypeStruct((16, D), BF),
        in_specs=[vm, vm] + [hb] * 6,
        out_specs=vm,
        scratch_shapes=scratch,
        name='moe',
        compiler_params=pltpu.CompilerParams(collective_id=cid, has_side_effects=True, vmem_limit_bytes=66_000_000),
    )(ue, h, ws1, ws3, ws2, w1, w3, w2)


def solution(mesh):
    rows = P(('ey', 'ex'))
    rep = P()

    def local(x, kv_k, kv_v, lens, topk_idx, gates, ln1, ln2, wq, wo, ws1, ws3, ws2, w1, w3, w2):
        h = _attn(x, kv_k, kv_v, lens, ln1, wq, wo)
        u = _rms(h, ln2)
        g1 = lax.reduce_precision(gates, 8, 7)
        r = gates - g1
        g2 = lax.reduce_precision(r, 8, 7)
        g3 = r - g2
        meta = jnp.concatenate([topk_idx.astype(F32), g1, g2, g3, jnp.zeros((16, MW - 32), F32)], axis=1).astype(BF)
        ue = jnp.concatenate([meta, u], axis=1)
        return _moe(64, 1, ue, h, ws1, ws3, ws2, w1, w3, w2)

    return jax.shard_map(
        local, mesh=mesh,
        in_specs=(rows, rows, rows, rows, rows, rows, rep, rep, rep, rep, rep, rep, rep, rows, rows, rows),
        out_specs=rows, check_vma=False)
```

time: 301 us -> 97.7 us (0.32)
  blocking collectives: 123 us -> 0 us
  Pallas kernels: 0 us -> 70.1 us
  waiting for transfers between devices: 64.1 us -> 0 us
  matrix products: 51.8 us -> 22.8 us
  local copies, waits for them, and re-layouts: 31.2 us -> 2.47 us
  between operations: 13.6 us -> 0.13 us
  other arithmetic: 12.1 us -> 1.85 us
  starting transfers between devices: 4.61 us -> 0 us
    all_gather x3 -> x0, blocking collectives: 94 us -> none  [the longest x1 32.4 us: local(): t_g = lax.all_gather(topk_idx, 'ey')]
    pallas_call x0 -> x1, Pallas kernels: none -> 70.1 us  [_moe(): pl.pallas_call(functools.partial(_moe_kernel, cap), out_shape=jax.ShapeDt...]
    reduce_scatter x1 -> x0, waiting for transfers between devices: 64.1 us -> none  [local(): lax.psum_scatter(partial[:ey * b].reshape(ey, b, d), 'ey', scatter_dimens...]
    all_to_all x1 -> x0, blocking collectives: 29 us -> none  [local(): recv = lax.all_to_all(send, 'ex', 0, 0)]
    dot_general x4 -> x0, matrix products: 28.1 us -> none  [the longest x1 14.4 us: _experts(): jnp.einsum('erf,efd->erd', z, w2, preferred_element_type=F32).astype(BF)]
    gather x4 -> x0, local copies, waits for them, and re-layouts: 13.1 us -> none  [the longest x3 6.66 us: _ranks(): return jnp.take_along_axis(before, topk, axis=-1)]
    scatter-add x1 -> x0, other arithmetic: 9.23 us -> none  [local(): jnp.zeros((ey * b + 1, d), F32).at[slot_tok]]
    scatter x2 -> x0, local copies, waits for them, and re-layouts: 8.83 us -> none  [the longest x1 4.52 us: local(): jnp.zeros((nslotv,), F32).at[pos].set(g_g.reshape(-1), mode='drop')]
  transfers between devices with their start and end apart: 2 -> 0, of which waited for: 1 -> 0; matrix products, arithmetic and copies ran while one was open for 2% -> 0% of each run, Pallas kernels for 0% -> 0%
where the time goes in v1:
time: 97.7 us; the launch traced here: 97.3 us
  Pallas kernels  70.1 us (72%)
  matrix products  22.8 us (23%)
  local copies, waits for them, and re-layouts  2.47 us (3%)
  other arithmetic  1.85 us (2%)
    pallas_call x1, Pallas kernels, _moe(): pl.pallas_call(functools.partial(_moe_kernel, cap), out_shape=jax.ShapeDt...  70.1 us
    dot_general x1, matrix products, _attn(): attn = jnp.dot(o.reshape(b, hq * dh), wo, preferred_element_type=F32)  8.18 us
    dot_general x1, matrix products, _attn(): jnp.dot(a, wq, preferred_element_type=F32).astype(BF)  8.15 us
    sub x1, matrix products, _attn(): p = jax.nn.softmax(s, axis=-1).astype(BF)  3.56 us
    dot_general x1, matrix products, _attn(): jnp.einsum('bkgl,blkd->bkgd', p, vv, preferred_element_type=F32).astype(BF)  2.93 us

profile of v1, /device:TPU:0, one launch (start us, length us, event | category | flops | bytes accessed | tf_op | source)
XLA Modules:
  0.0 97.3 jit_solution(5623599856364696400)
XLA Ops:
  0.0 0.7 convert_element_type.37
  0.7 1.0 fusion.22
  1.7 8.1 %fusion.17 = bf16[2,8,32,128]{3,1,2,0:T(8,128)(2,1)S(1)} fusion(bf16[2048,4096]{1,0:T(8,128)(2,1)} %param.24, bf16[16,2048]{1,0:T(8,128)(2,1)} %param.16, f32[2048]{0:T(1024)S(1)} %convert_element_type.37, f32[16]{0:T(128)S(1)} %add_rsqrt_fusion.1), kind=kOutput, calls=%fused_computation.13 | convolution fusion | flops 268632064 | bytes 16982080 | tf_op jit(solution)/shard_map/dot_general | solution.py:34
  9.9 0.0 copy-done.5
  9.9 0.1 iota_compare_fusion
  9.9 3.6 %fusion.31 = (f32[16,4,8]{2,1,0:T(4,128)S(1)}, f32[16,4,8,256]{3,2,1,0:T(8,128)S(1)}) fusion(bf16[16,4,8,128]{3,2,1,0:T(8,128)(2,1)S(1)} %bitcast.15, bf16[16,256,4,128]{3,2,1,0:T(4,128)(2,1)} %param.17, pred[16,256]{1,0:T(8,128)(4,1)S(1)} %iota_compare_fusion), kind=kOutput, calls=%fused_computation.36 | convolution fusion | flops 34078976 | bytes 4855808 | tf_op jit(solution)/shard_map/sub | solution.py:38
  13.5 0.0 copy-start
  13.5 2.9 %fusion.14 = bf16[16,4,8,128]{3,2,1,0:T(8,128)(2,1)S(1)} fusion(bf16[16,256,4,128]{3,2,1,0:T(4,128)(2,1)} %param.18, f32[16,4,8,256]{3,2,1,0:T(8,128)S(1)} %get-tuple-element.9, f32[16,4,8]{2,1,0:T(4,128)S(1)} %get-tuple-element.8), kind=kOutput, calls=%fused_computation.12 | convolution fusion | flops 33882112 | bytes 4851712 | tf_op jit(solution)/shard_map/bkgl,blkd->bkgd/dot_general | solution.py:39
  16.4 0.0 copy-done
  16.4 0.0 copy-start.3
  16.4 0.0 copy-start.2
  16.5 0.0 copy-start.4
  16.5 8.2 %fusion.19 = (f32[16]{0:T(128)S(1)}, bf16[16,2048]{1,0:T(8,128)(2,1)S(1)}) fusion(bf16[4096,2048]{1,0:T(8,128)(2,1)} %param.25, bf16[2,8,32,128]{3,2,1,0:T(8,128)(2,1)S(1)} %bitcast.14, bf16[16,2048]{1,0:T(8,128)(2,1)S(1)} %copy-done), kind=kOutput, calls=%fused_computation.20 | convolution fusion | flops 268632064 | bytes 17039424 | tf_op jit(solution)/shard_map/dot_general | solution.py:40
  24.6 0.0 copy-start.1
  24.7 0.0 copy-done.3
  24.7 0.1 fusion.21
  24.8 0.0 copy-done.2
  24.8 0.1 copy.23
  24.9 0.1 copy.24
  25.0 0.1 copy.22
  25.1 0.7 concatenate.6.ue_ref
  25.8 0.0 copy-done.1
  25.8 70.1 %moe.1 = bf16[16,2048]{1,0:T(8,128)(2,1)} custom-call(bf16[16,2176]{1,0:T(8,128)(2,1)} %concatenate.6.ue_ref, bf16[16,2048]{1,0:T(8,128)(2,1)} %copy-done.1, bf16[2048,768]{1,0:T(8,128)(2,1)} %ws1.1, bf16[2048,768]{1,0:T(8,128)(2,1)} %ws3.1, bf16[768,2048]{1,0:T(8,128)(2,1)} %ws2.1, bf16[4,2048,768]{2,1,0:T(8,128)(2,1)} %w1.1, bf16[4,2048,768]{2,1,0:T(8,128)(2,1)} %w3.1, ...), custom_call_target="tpu_custom_call" | custom-call | tf_op jit(solution)/shard_map/moe/pallas_call | solution.py:289
  95.9 1.5 %copy.49 = bf16[16,2048]{1,0:T(8,128)(2,1)} copy(bf16[16,2048]{1,0:T(8,128)(2,1)} %moe.1) | data formatting | bytes 131072
  (10 shorter events, 0.1 us)
Async XLA Ops:
  1.7 8.2 %copy-start.5 = (s32[16]{0:T(128)S(1)}, s32[16]{0:T(128)}, u32[]{:S(2)}) copy-start(s32[16]{0:T(128)} %param.19) | copy-start | bytes 196
  13.5 2.9 %copy-start = (bf16[16,2048]{1,0:T(8,128)(2,1)S(1)}, bf16[16,2048]{1,0:T(8,128)(2,1)}, u32[]{:S(2)}) copy-start(bf16[16,2048]{1,0:T(8,128)(2,1)} %param.16) | copy-start | bytes 196612
  16.4 8.2 %copy-start.3 = (bf16[2048]{0:T(1024)(128)(2,1)S(1)}, bf16[2048]{0:T(1024)(128)(2,1)}, u32[]{:S(2)}) copy-start(bf16[2048]{0:T(1024)(128)(2,1)} %param.23) | copy-start | bytes 12292
  16.4 8.3 %copy-start.2 = (f32[16,8]{0,1:T(8,128)S(1)}, f32[16,8]{0,1:T(8,128)}, u32[]{:S(2)}) copy-start(f32[16,8]{0,1:T(8,128)} %param.21) | copy-start | bytes 1540
  16.5 8.5 %copy-start.4 = (s32[16,8]{0,1:T(8,128)S(1)}, s32[16,8]{0,1:T(8,128)}, u32[]{:S(2)}) copy-start(s32[16,8]{0,1:T(8,128)} %param.20) | copy-start | bytes 1540
  24.6 1.1 %copy-start.1 = (bf16[16,2048]{1,0:T(8,128)(2,1)}, bf16[16,2048]{1,0:T(8,128)(2,1)S(1)}, u32[]{:S(2)}) copy-start(bf16[16,2048]{1,0:T(8,128)(2,1)S(1)} %get-tuple-element.11.h_ref) | copy-start | bytes 196612

commit v2 on v1

v2 whole, which is shorter than its diff:
```python
import functools

import jax
import jax.numpy as jnp
from jax import lax
from jax.experimental import pallas as pl
from jax.experimental.pallas import tpu as pltpu
from jax.sharding import PartitionSpec as P

EPS = 1e-6
BF = jnp.bfloat16
F32 = jnp.float32
I32 = jnp.int32

D = 2048
FF = 768
NT = 512
CAPE = 4
NC = 4
CW = D // NC
MW = 128


def _rms(v, w):
    v = v.astype(F32)
    r = lax.rsqrt(jnp.mean(v * v, axis=-1, keepdims=True) + EPS)
    return (v * r * w.astype(F32)).astype(BF)


def _split3(v):
    a = v.astype(BF)
    r = v - a.astype(F32)
    b = r.astype(BF)
    c = (r - b.astype(F32)).astype(BF)
    return a, b, c


def _dot(a, b):
    return jnp.dot(a, b, preferred_element_type=F32)


def _dot_tt(a, b):
    return lax.dot_general(a, b, (((1,), (1,)), ((), ())), preferred_element_type=F32)


def _dot_00(a, b):
    return lax.dot_general(a, b, (((0,), (0,)), ((), ())), preferred_element_type=F32)


def _rcopy(src, dst, s, r, d):
    return pltpu.make_async_remote_copy(src_ref=src, dst_ref=dst, send_sem=s, recv_sem=r,
                                        device_id=d, device_id_type=pl.DeviceIdType.MESH)


class _Pos:
    def __init__(self):
        self.iy = iy = lax.axis_index('ey')
        self.ix = ix = lax.axis_index('ex')
        self.z, self.y = iy // 2, iy % 2
        self.x, self.k = ix // 2, ix % 2
        self.ydev = (self.z * 2 + (1 - self.y), ix)
        self.xdev = (iy, (1 - self.x) * 2 + self.k)
        self.kdev = (iy, self.x * 2 + (1 - self.k))

    def zdev(self, d):
        return (((self.z + d) % 4) * 2 + self.y, self.ix)

    def greet(self):
        barrier = pltpu.get_barrier_semaphore()
        for d in (self.zdev(1), self.zdev(2), self.zdev(3), self.ydev, self.xdev, self.kdev):
            pl.semaphore_signal(barrier, inc=1, device_id=d, device_id_type=pl.DeviceIdType.MESH)
        return barrier


QC = 8
OC = 4


def _attn_kernel(cap, x_ref, meta_ref, lens_ref, ln1_ref, ln2_ref, wq, wo, kk, vv,
                 h_ref, u_ref, mt_ref, flag_ref,
                 wqb, wob, kb, vb, qs, os_, mall,
                 qsem, osem, ksem, vsem, ags, agr):
    p = _Pos()
    z, y, x, k = p.z, p.y, p.x, p.k
    barrier = p.greet()

    def qcp(c):
        return pltpu.make_async_copy(wq.at[:, pl.ds(pl.multiple_of(c * 512, 512), 512)], wqb.at[c], qsem.at[c])

    def ocp(c):
        return pltpu.make_async_copy(wo.at[:, pl.ds(pl.multiple_of(c * 512, 512), 512)], wob.at[c], osem.at[c])

    def kcp(t):
        return pltpu.make_async_copy(kk.at[pl.ds(t * 4, 4)], kb.at[pl.ds(t * 4, 4)], ksem.at[t])

    def vcp(t):
        return pltpu.make_async_copy(vv.at[pl.ds(t * 4, 4)], vb.at[pl.ds(t * 4, 4)], vsem.at[t])

    for c in range(QC):
        qcp(c).start()
    for t in range(4):
        kcp(t).start()
        vcp(t).start()
    for c in range(OC):
        ocp(c).start()

    mall[z, y, x, k] = meta_ref[...]
    a = _rms(x_ref[...], ln1_ref[...])
    pl.semaphore_wait(barrier, 6)
    zc = [_rcopy(meta_ref, mall.at[z, y, x, k], ags.at[d - 1], agr.at[d - 1], p.zdev(d)) for d in (1, 2, 3)]
    for cp in zc:
        cp.start()

    def qstep(c, _):
        qcp(c).wait()
        q = _dot(a, wqb[c]).astype(BF).astype(F32)
        for j in range(4):
            qs[pl.ds(pl.multiple_of(c * 64 + j * 16, 16), 16), :] = q[:, j * 128:(j + 1) * 128]
        return 0
    lax.fori_loop(0, QC, qstep, 0)

    for cp in zc:
        cp.wait_recv()
    yb = mall.at[:, y, x, k]
    yc = _rcopy(yb, yb, ags.at[3], agr.at[3], p.ydev)
    yc.start()
    xb = mall.at[:, :, x, k]
    xc = _rcopy(xb, xb, ags.at[4], agr.at[4], p.xdev)
    kb_ = mall.at[:, :, :, k]
    kc = _rcopy(kb_, kb_, ags.at[5], agr.at[5], p.kdev)

    col = lax.broadcasted_iota(I32, (32, 1024), 1)
    row = lax.broadcasted_iota(I32, (32, 1024), 0)
    headok = (col % 4) == (row // 8)
    pos = jnp.where(headok, col // 4, 1 << 20)

    def astep(g, _):
        kcp(g).wait()
        vcp(g).wait()
        for j in range(4):
            t = g * 4 + j
            q = qs[pl.ds(t, 32, stride=16), :].astype(BF)
            s = _dot_tt(q, kb[t]) * 128.0 ** -0.5
            s = jnp.where(pos < lens_ref[t], s, -jnp.inf)
            m = jnp.max(s, axis=1, keepdims=True)
            e = jnp.exp(s - m)
            pr = (e / jnp.sum(e, axis=1, keepdims=True)).astype(BF)
            o = _dot(pr, vb[t])
            os_[pl.ds(t, 32, stride=16), :] = o

        @pl.when(g == 1)
        def _():
            yc.wait_recv()
            xc.start()

        @pl.when(g == 3)
        def _():
            xc.wait_recv()
            kc.start()
        return 0
    lax.fori_loop(0, 4, astep, 0)

    oo = jnp.concatenate([os_[h * 16:(h + 1) * 16, :] for h in range(32)], axis=1).astype(BF)

    def ostep(c, _):
        ocp(c).wait()
        sl = pl.ds(pl.multiple_of(c * 512, 512), 512)
        h_ref[:, sl] = (x_ref[:, sl].astype(F32) + _dot(oo, wob[c])).astype(BF)
        return 0
    lax.fori_loop(0, OC, ostep, 0)
    u_ref[...] = _rms(h_ref[...], ln2_ref[...])

    kc.wait_recv()
    mt = mall[...].reshape(NT, MW).astype(F32).T[0:32]
    mt_ref[...] = mt
    tk = mt[0:8]
    rm = jnp.concatenate([jnp.max(jnp.where((tk >= 16.0 * r) & (tk < 16.0 * r + 16.0), 1.0, 0.0), axis=0, keepdims=True)
                          for r in range(8)], axis=0)
    gt = (lax.broadcasted_iota(I32, (NT, 128), 0) // 16) % 8
    gsel = (gt == lax.broadcasted_iota(I32, (NT, 128), 1)).astype(F32).astype(BF)
    cnt = _dot(rm.astype(BF), gsel)
    flag_ref[...] = jnp.broadcast_to(jnp.max(cnt, axis=(0, 1), keepdims=True), (8, 128))
    for cp in zc + [yc, xc, kc]:
        cp.wait_send()


def _attn(cap, x, meta, lens, ln1, ln2, wq, wo, kk, vv):
    vm = pl.BlockSpec(memory_space=pltpu.VMEM)
    hb = pl.BlockSpec(memory_space=pl.ANY)
    return pl.pallas_call(
        functools.partial(_attn_kernel, cap),
        out_shape=(jax.ShapeDtypeStruct((16, D), BF), jax.ShapeDtypeStruct((16, D), BF),
                   jax.ShapeDtypeStruct((32, NT), F32), jax.ShapeDtypeStruct((8, 128), F32)),
        in_specs=[vm, vm, pl.BlockSpec(memory_space=pltpu.SMEM), vm, vm] + [hb] * 4,
        out_specs=(vm, vm, vm, vm),
        scratch_shapes=[
            pltpu.VMEM((QC, D, 512), BF), pltpu.VMEM((OC, 4096, 512), BF),
            pltpu.VMEM((16, 1024, 128), BF), pltpu.VMEM((16, 1024, 128), BF),
            pltpu.VMEM((512, 128), F32), pltpu.VMEM((512, 128), F32), pltpu.VMEM((4, 2, 2, 2, 16, MW), BF),
            pltpu.SemaphoreType.DMA((QC,)), pltpu.SemaphoreType.DMA((OC,)),
            pltpu.SemaphoreType.DMA((4,)), pltpu.SemaphoreType.DMA((4,)),
            pltpu.SemaphoreType.DMA((6,)), pltpu.SemaphoreType.DMA((6,)),
        ],
        name='attn',
        compiler_params=pltpu.CompilerParams(collective_id=3, has_side_effects=True, vmem_limit_bytes=60_000_000),
    )(x, meta, lens, ln1, ln2, wq, wo, kk, vv)


def _moe_kernel(cap, u_ref, h_ref, mt_ref, ws1, ws3, ws2, w1, w3, w2, out_ref,
                zb, yb, uc, wa, wb, wc, xe, zz, fc, gm, pm, lmat,
                ps, ra, rx, ry, dz_buf, rz, base,
                wsem, ags, agr, cbs, cbr):
    p = _Pos()
    iy, ix, z, y, x, k = p.iy, p.ix, p.z, p.y, p.x, p.k
    dev = iy * 4 + ix
    barrier = p.greet()

    def wcp(e, i):
        return pltpu.make_async_copy((w1, w3, w2)[i].at[e], (wa, wb, wc)[i].at[(e + 1) % 4], wsem.at[e, i])
    scp = [pltpu.make_async_copy(s, b.at[0], wsem.at[4, i]) for i, (s, b) in enumerate(((ws1, wa), (ws3, wb), (ws2, wc)))]
    for cp in scp:
        cp.start()
    for e in range(3):
        wcp(e, 0).start()
        wcp(e, 1).start()
    for e in range(3):
        wcp(e, 2).start()

    pl.semaphore_wait(barrier, 6)
    zc = []
    for c in range(NC):
        src = u_ref.at[:, pl.ds(CW * c, CW)]
        cps = [_rcopy(src, zb.at[c, z], ags.at[c, d - 1], agr.at[c, d - 1], p.zdev(d)) for d in (1, 2, 3)]
        for cp in cps:
            cp.start()
        zc.append(cps)
        zb[c, z] = u_ref[:, CW * c:CW * (c + 1)]

    tk = mt_ref[0:8]
    gts = (mt_ref[8:16], mt_ref[16:24], mt_ref[24:32])
    blk1 = lax.broadcasted_iota(I32, (1, NT), 1) // 16
    ti = lax.broadcasted_iota(I32, (NT, NT), 0)
    tj = lax.broadcasted_iota(I32, (NT, NT), 1)
    earlier = ti < tj
    lmat[...] = jnp.where(earlier & ((ti // 16) % 8 == (tj // 16) % 8), 1.0, 0.0).astype(BF)

    def rowmatch(r):
        lo = (r * 16).astype(F32)
        return jnp.max(jnp.where((tk >= lo) & (tk < lo + 16.0), 1.0, 0.0), axis=0, keepdims=True)
    rm = jnp.concatenate([rowmatch(iy), rowmatch(z * 2 + (1 - y)), jnp.zeros((6, NT), F32)], axis=0)
    rb = _dot(rm.astype(BF), lmat[...])
    ridx = jnp.where((rm > 0.5) & (rb < cap - 0.5), rb, -1.0)
    gidx = ((blk1 % 2) * 2 + (blk1 // 2) % 2) * 2 + (blk1 // 4) % 2
    mine = gidx == (k * 2 + x) * 2 + y
    ci = lax.broadcasted_iota(I32, (cap, NT), 0).astype(F32)
    own = jnp.concatenate([(ci == jnp.where(mine, ridx[0:1], -1.0)).astype(F32),
                           (ci == jnp.where(mine, ridx[1:2], -1.0)).astype(F32)], axis=0).astype(BF)
    sj = lax.broadcasted_iota(I32, (NT, 64), 1)
    st = lax.broadcasted_iota(I32, (NT, 64), 0)
    sel = (st == (sj // 16) * 128 + y * 64 + ix * 16 + sj % 16).astype(F32).astype(BF)
    emat = _dot(own, sel).astype(BF)

    yc = []
    for c in range(NC):
        for cp in zc[c]:
            cp.wait_recv()
        lst = _dot(emat, zb[c].reshape(64, CW)).astype(BF)
        yb[c] = lst[cap:]
        cp = _rcopy(yb.at[c], uc.at[c, k, x, y], ags.at[c, 3], agr.at[c, 3], p.ydev)
        cp.start()
        yc.append(cp)
        uc[c, k, x, y] = lst[:cap]

    scp[0].wait()
    scp[1].wait()
    u = u_ref[...]
    g = _dot(u, wa[0])
    v = _dot(u, wb[0])
    zs = (jax.nn.silu(g) * v).astype(BF)

    xc = []
    for c in range(NC):
        yc[c].wait_recv()
        cp = _rcopy(uc.at[c, k, x], uc.at[c, k, x], ags.at[c, 4], agr.at[c, 4], p.xdev)
        cp.start()
        xc.append(cp)

    scp[2].wait()
    base[...] = h_ref[...].astype(F32) + _dot(zs, wc[0]).astype(BF).astype(F32)
    for i in range(3):
        wcp(3, i).start()

    lmat[...] = jnp.where(earlier & (ti // 16 == tj // 16), 1.0, 0.0).astype(BF)
    ms, gs = [], []
    for e in range(4):
        eq = tk == (dev * 4 + e).astype(F32)
        ms.append(jnp.sum(jnp.where(eq, 1.0, 0.0), axis=0, keepdims=True))
        gs.append([jnp.sum(jnp.where(eq, gg, 0.0), axis=0, keepdims=True) for gg in gts])
    mstack = jnp.concatenate(ms + [jnp.zeros((4, NT), F32)], axis=0)
    before = _dot(mstack.astype(BF), lmat[...])
    slot = jnp.where((mstack > 0.5) & (before < CAPE - 0.5), (blk1 * CAPE).astype(F32) + before, -1.0)
    cidx = jnp.where(ridx[0:1] > -0.5, (gidx * cap).astype(F32) + ridx[0:1], -1.0)
    cmat = (lax.broadcasted_iota(I32, (8 * cap, NT), 0).astype(F32) == cidx).astype(F32).astype(BF)
    si = lax.broadcasted_iota(I32, (128, NT), 0).astype(F32)
    for e in range(4):
        hit = si == slot[e:e + 1]
        pm[128 * e:128 * (e + 1), :] = _dot_tt(hit.astype(F32).astype(BF), cmat).astype(BF)
        for m in range(3):
            gp = jnp.where(hit, gs[e][m], 0.0).astype(BF)
            gm[m, :, 128 * e:128 * (e + 1)] = _dot_tt(cmat, gp).astype(BF)

    kc = []
    for c in range(NC):
        xc[c].wait_recv()
        cp = _rcopy(uc.at[c, k], uc.at[c, k], ags.at[c, 5], agr.at[c, 5], p.kdev)
        cp.start()
        kc.append(cp)
    for c in range(NC):
        kc[c].wait_recv()
        xe[:, :, c * CW:(c + 1) * CW] = _dot(pm[...], uc[c].reshape(8 * cap, CW)).astype(BF).reshape(4, 128, CW)

    def ffn(e, _):
        s = (e + 1) % 4
        wcp(e, 0).wait()
        g = _dot(xe[e], wa[s])
        wcp(e, 1).wait()
        v = _dot(xe[e], wb[s])
        zz[e] = (jax.nn.silu(g) * v).astype(BF)
        return 0
    lax.fori_loop(0, 4, ffn, 0)
    for e in range(4):
        wcp(e, 2).wait()

    ca, cx, cy, cz = {}, {}, {}, {}

    def stage0(c):
        for e in range(4):
            fc[128 * e:128 * (e + 1), :] = _dot(zz[e], wc[(e + 1) % 4, :, c * CW:(c + 1) * CW]).astype(BF)
        f = fc[...]
        o = _dot(gm[0], f) + _dot(gm[1], f) + _dot(gm[2], f)
        ps[c] = o.reshape(2, 2, 2, cap, CW)
        ca[c] = _rcopy(ps.at[c, 1 - k], ra.at[c], cbs.at[c, 0], cbr.at[c, 0], p.kdev)
        ca[c].start()

    def stage1(c):
        ca[c].wait_recv()
        ps[c, k] = ps[c, k] + ra[c]
        cx[c] = _rcopy(ps.at[c, k, 1 - x], rx.at[c], cbs.at[c, 1], cbr.at[c, 1], p.xdev)
        cx[c].start()

    def stage2(c):
        cx[c].wait_recv()
        ps[c, k, x] = ps[c, k, x] + rx[c]
        cy[c] = _rcopy(ps.at[c, k, x, 1 - y], ry.at[c], cbs.at[c, 2], cbr.at[c, 2], p.ydev)
        cy[c].start()

    def stage3(c):
        cy[c].wait_recv()
        data = jnp.concatenate([ps[c, k, x, y], ry[c]], axis=0)
        a, b, d = _split3(data)
        dn = _dot_00(emat, a) + _dot_00(emat, b) + _dot_00(emat, d)
        dz_buf[c] = dn.reshape(4, 16, CW)
        cz[c] = [_rcopy(dz_buf.at[c, (z + d) % 4], rz.at[c, d - 1], cbs.at[c, 2 + d], cbr.at[c, 2 + d], p.zdev(d))
                 for d in (1, 2, 3)]
        for cp in cz[c]:
            cp.start()

    def stage4(c):
        for cp in cz[c]:
            cp.wait_recv()
        o = base[:, c * CW:(c + 1) * CW] + dz_buf[c, z] + rz[c, 0] + rz[c, 1] + rz[c, 2]
        out_ref[:, c * CW:(c + 1) * CW] = o.astype(BF)

    stages = (stage0, stage1, stage2, stage3, stage4)
    for step in range(NC + 4):
        for s, fn in enumerate(stages):
            c = step - s
            if 0 <= c < NC:
                fn(c)
    for c in range(NC):
        for cp in zc[c] + [yc[c], xc[c], kc[c], ca[c], cx[c], cy[c]] + cz[c]:
            cp.wait_send()


def _moe(cap, cid, u, h, mt, ws1, ws3, ws2, w1, w3, w2):
    vm = pl.BlockSpec(memory_space=pltpu.VMEM)
    hb = pl.BlockSpec(memory_space=pl.ANY)
    scratch = [
        pltpu.VMEM((NC, 4, 16, CW), BF), pltpu.VMEM((NC, cap, CW), BF), pltpu.VMEM((NC, 2, 2, 2, cap, CW), BF),
        pltpu.VMEM((4, D, FF), BF), pltpu.VMEM((4, D, FF), BF), pltpu.VMEM((4, FF, D), BF),
        pltpu.VMEM((4, 128, D), BF), pltpu.VMEM((4, 128, FF), BF), pltpu.VMEM((512, CW), BF),
        pltpu.VMEM((3, 8 * cap, 512), BF), pltpu.VMEM((512, 8 * cap), BF), pltpu.VMEM((NT, NT), BF),
        pltpu.VMEM((NC, 2, 2, 2, cap, CW), F32), pltpu.VMEM((NC, 2, 2, cap, CW), F32),
        pltpu.VMEM((NC, 2, cap, CW), F32), pltpu.VMEM((NC, cap, CW), F32),
        pltpu.VMEM((NC, 4, 16, CW), F32), pltpu.VMEM((NC, 3, 16, CW), F32),
        pltpu.VMEM((16, D), F32),
        pltpu.SemaphoreType.DMA((5, 3)), pltpu.SemaphoreType.DMA((NC, 6)), pltpu.SemaphoreType.DMA((NC, 6)),
        pltpu.SemaphoreType.DMA((NC, 6)), pltpu.SemaphoreType.DMA((NC, 6)),
    ]
    return pl.pallas_call(
        functools.partial(_moe_kernel, cap),
        out_shape=jax.ShapeDtypeStruct((16, D), BF),
        in_specs=[vm, vm, vm] + [hb] * 6,
        out_specs=vm,
        scratch_shapes=scratch,
        name='moe',
        compiler_params=pltpu.CompilerParams(collective_id=cid, has_side_effects=True, vmem_limit_bytes=66_000_000),
    )(u, h, mt, ws1, ws3, ws2, w1, w3, w2)


CAP = 32


def solution(mesh):
    rows = P(('ey', 'ex'))
    rep = P()

    def local(x, kv_k, kv_v, lens, topk_idx, gates, ln1, ln2, wq, wo, ws1, ws3, ws2, w1, w3, w2):
        g1 = lax.reduce_precision(gates, 8, 7)
        r = gates - g1
        g2 = lax.reduce_precision(r, 8, 7)
        g3 = r - g2
        meta = jnp.concatenate([topk_idx.astype(F32), g1, g2, g3, jnp.zeros((16, MW - 32), F32)], axis=1).astype(BF)
        h, u, mt, cnt = _attn(CAP, x, meta, lens, ln1[None], ln2[None], wq, wo,
                              kv_k.reshape(16, 1024, 128), kv_v.reshape(16, 1024, 128))
        args = (u, h, mt, ws1, ws3, ws2, w1, w3, w2)
        return lax.cond(cnt[0, 0] > CAP + 0.5, functools.partial(_moe, 64, 2), functools.partial(_moe, CAP, 1), *args)

    return jax.shard_map(
        local, mesh=mesh,
        in_specs=(rows, rows, rows, rows, rows, rows, rep, rep, rep, rep, rep, rep, rep, rows, rows, rows),
        out_specs=rows, check_vma=False)
```

time: 97.7 us -> 84 us (0.86)
  matrix products: 22.8 us -> 0 us
  Pallas kernels: 70.1 us -> 75.3 us
  local copies, waits for them, and re-layouts: 2.47 us -> 6 us
    pallas_call x0 -> x1, Pallas kernels: none -> 25.2 us  [_attn(): pl.pallas_call(functools.partial(_attn_kernel, cap), out_shape=(jax.Shape...]
    pallas_call x1, Pallas kernels: 70.1 us -> 50.2 us  [_moe(): pl.pallas_call(functools.partial(_moe_kernel, cap), out_shape=jax.ShapeDt...]
    dot_general x3 -> x0, matrix products: 19.2 us -> none  [the longest x1 8.18 us: _attn(): attn = jnp.dot(o.reshape(b, hq * dh), wo, preferred_element_type=F32)]
    sub x1 -> x0, matrix products: 3.56 us -> none  [_attn(): p = jax.nn.softmax(s, axis=-1).astype(BF)]
    broadcast_in_dim x0 -> x2, local copies, waits for them, and re-layouts: none -> 2.57 us  [the longest x1 1.29 us: local(): ln1[None]]
    slice x0 -> x1, local copies, waits for them, and re-layouts: none -> 1.2 us  [local(): cnt[0, 0] > CAP + 0.5]
where the time goes in v2:
time: 84 us; the launch traced here: 83.6 us
  Pallas kernels  75.3 us (90%)
  local copies, waits for them, and re-layouts  6 us (7%)
  other arithmetic  1.39 us (2%)
    pallas_call x1, Pallas kernels, _moe(): pl.pallas_call(functools.partial(_moe_kernel, cap), out_shape=jax.ShapeDt...  50.2 us
    pallas_call x1, Pallas kernels, _attn(): pl.pallas_call(functools.partial(_attn_kernel, cap), out_shape=(jax.Shape...  25.2 us

profile of v2, /device:TPU:0, one launch (start us, length us, event | category | flops | bytes accessed | tf_op | source)
XLA Modules:
  0.0 83.6 jit_solution(17541259913466436386)
XLA Ops:
  0.0 0.7 convert_element_type.10
  0.7 0.1 copy.22
  0.8 0.7 reduce_precision.6
  1.5 0.1 copy.23
  1.5 1.3 %broadcast_in_dim.10.ln1_ref = bf16[1,2048]{1,0:T(2,128)(2,1)} reshape(bf16[2048]{0:T(1024)(128)(2,1)} %param.24) | data formatting | bytes 8192 | tf_op jit(solution)/shard_map/broadcast_in_dim | solution.py:424
  2.8 1.3 %broadcast_in_dim.11.ln2_ref = bf16[1,2048]{1,0:T(2,128)(2,1)} reshape(bf16[2048]{0:T(1024)(128)(2,1)} %param.25) | data formatting | bytes 8192 | tf_op jit(solution)/shard_map/broadcast_in_dim | solution.py:424
  4.1 0.8 copy.24
  4.9 0.7 concatenate.4.meta_ref
  5.6 25.2 %attn.1 = (bf16[16,2048]{1,0:T(8,128)(2,1)S(1)}, bf16[16,2048]{1,0:T(8,128)(2,1)S(1)}, f32[32,512]{1,0:T(8,128)S(1)}, f32[8,128]{1,0:T(8,128)}) custom-call(bf16[16,2048]{1,0:T(8,128)(2,1)} %x_ref.1, bf16[16,128]{1,0:T(8,128)(2,1)} %concatenate.4.meta_ref, s32[16]{0:T(128)} %lens_ref.1, bf16[1,2048]{1,0:T(2,128)(2,1)} %broadcast_in_dim.10.ln1_ref, ...), custom_call_target="tpu_custom_call" | custom-call | tf_op jit(solution)/shard_map/attn/pallas_call | solution.py:190
  30.7 1.2 %slice.3 = f32[1,1]{1,0:T(1,128)} slice(f32[8,128]{1,0:T(8,128)} %get-tuple-element.66), slice={[0:1], [0:1]} | slice | bytes 8 | tf_op jit(solution)/shard_map/slice | solution.py:427
  32.6 50.4 %conditional.1 = (bf16[16,2048]{1,0:T(8,128)(2,1)S(1)}) conditional(s32[]{:T(128)} %bitcast.2, (bf16[16,2048]{1,0:T(8,128)(2,1)S(1)}, bf16[16,2048]{1,0:T(8,128)(2,1)S(1)}, f32[32,512]{1,0:T(8,128)S(1)}, bf16[2048,768]{1,0:T(8,128)(2,1)}, bf16[2048,768]{1,0:T(8,128)(2,1)}, /*index=5*/bf16[768,2048]{1,0:T(8,128)(2,1)}, ...), branch_computations={%region_0.0_spmd, %region_1.0_spmd} | conditional | bytes 8 | solution.py:427
  32.6 50.2 %moe.2 = bf16[16,2048]{1,0:T(8,128)(2,1)S(1)} custom-call(bf16[16,2048]{1,0:T(8,128)(2,1)S(1)} %get-tuple-element.44.u_ref, bf16[16,2048]{1,0:T(8,128)(2,1)S(1)} %get-tuple-element.45.h_ref, f32[32,512]{1,0:T(8,128)S(1)} %get-tuple-element.46.mt_ref, bf16[2048,768]{1,0:T(8,128)(2,1)} %get-tuple-element.47.ws1, bf16[2048,768]{1,0:T(8,128)(2,1)} %get-tuple-element.48.ws3, ...), custom_call_target="tpu_custom_call" | custom-call | tf_op jit(solution)/shard_map/cond/branch_0_fun/moe/pallas_call | solution.py:400
  83.0 0.6 copy.29
  (2 shorter events, 0.0 us)

commit v3 on v2

v3 whole, which is shorter than its diff:
```python
import functools

import jax
import jax.numpy as jnp
from jax import lax
from jax.experimental import pallas as pl
from jax.experimental.pallas import tpu as pltpu
from jax.sharding import PartitionSpec as P

EPS = 1e-6
BF = jnp.bfloat16
F32 = jnp.float32
I32 = jnp.int32

D = 2048
FF = 768
NT = 512
CAPE = 4
NC = 4
CW = D // NC
CC = 4
CX = D // CC
MW = 128


def _rms(v, w):
    v = v.astype(F32)
    r = lax.rsqrt(jnp.mean(v * v, axis=-1, keepdims=True) + EPS)
    return (v * r * w.astype(F32)).astype(BF)


def _split3(v):
    a = v.astype(BF)
    r = v - a.astype(F32)
    b = r.astype(BF)
    c = (r - b.astype(F32)).astype(BF)
    return a, b, c


def _dot(a, b):
    return jnp.dot(a, b, preferred_element_type=F32)


def _dot_tt(a, b):
    return lax.dot_general(a, b, (((1,), (1,)), ((), ())), preferred_element_type=F32)


def _dot_00(a, b):
    return lax.dot_general(a, b, (((0,), (0,)), ((), ())), preferred_element_type=F32)


def _rcopy(src, dst, s, r, d):
    return pltpu.make_async_remote_copy(src_ref=src, dst_ref=dst, send_sem=s, recv_sem=r,
                                        device_id=d, device_id_type=pl.DeviceIdType.MESH)


class _Pos:
    def __init__(self):
        self.iy = iy = lax.axis_index('ey')
        self.ix = ix = lax.axis_index('ex')
        self.z, self.y = iy // 2, iy % 2
        self.x, self.k = ix // 2, ix % 2
        self.ydev = (self.z * 2 + (1 - self.y), ix)
        self.xdev = (iy, (1 - self.x) * 2 + self.k)
        self.kdev = (iy, self.x * 2 + (1 - self.k))

    def zdev(self, d):
        return (((self.z + d) % 4) * 2 + self.y, self.ix)

    def far(self, d):
        return (((self.z + d) % 4) * 2 + 1 - self.y, self.ix)

    def greet(self):
        barrier = pltpu.get_barrier_semaphore()
        for d in self.column() + self.row():
            pl.semaphore_signal(barrier, inc=1, device_id=d, device_id_type=pl.DeviceIdType.MESH)
        return barrier

    def column(self):
        return [self.zdev(d) for d in range(1, 4)] + [self.far(d) for d in range(4)]

    def row(self):
        return [(self.iy, (self.ix + d) % 4) for d in range(1, 4)]


def _layer_kernel(cap, capc, win_ref, x_ref, topk_ref, gates_ref, lens_ref, ln1_ref, ln2_ref,
                  wq, wo, kk, vv, ws1, ws3, ws2, w1, w3, w2, out_ref, flag_ref,
                  g1b, g2b, kb, vb, qs, os_, mall, mscr, mt_ref, u_ref,
                  zb, yb, uc, xe, zz, fc, gm, pm, ps, ra, rx, ry, dz_buf, rz, base,
                  qsem, osem, ksem, vsem, esem, mgs, mgr, ags, agr, cbs, cbr):
    p = _Pos()
    iy, ix, z, y, x, k = p.iy, p.ix, p.z, p.y, p.x, p.k
    dev = iy * 4 + ix
    barrier = p.greet()

    def qcp(c):
        sl = pl.ds(pl.multiple_of(c * 512, 512), 512)
        return pltpu.make_async_copy(wq.at[:, sl], g1b.at[:, sl], qsem.at[c])

    def ocp(c):
        sl = pl.ds(pl.multiple_of(c * 512, 512), 512)
        return pltpu.make_async_copy(wo.at[sl], g2b.at[sl], osem.at[c])

    def kcp(t):
        return pltpu.make_async_copy(kk.at[pl.ds(t * 4, 4)], kb.at[pl.ds(t * 4, 4)], ksem.at[t])

    def vcp(t):
        return pltpu.make_async_copy(vv.at[pl.ds(t * 4, 4)], vb.at[pl.ds(t * 4, 4)], vsem.at[t])

    def col13(e, i):
        return pl.ds(pl.multiple_of((2 * e + i) * FF, 256), FF)

    def wcp(e, i):
        if i == 2:
            return pltpu.make_async_copy(w2.at[e], g2b.at[pl.ds(pl.multiple_of(e * FF, 256), FF)], esem.at[e, 2])
        return pltpu.make_async_copy((w1, w3)[i].at[e], g1b.at[:, col13(e, i)], esem.at[e, i])
    scp = [pltpu.make_async_copy(ws1, g1b.at[:, col13(3, 0)], esem.at[4, 0]),
           pltpu.make_async_copy(ws3, g1b.at[:, col13(3, 1)], esem.at[4, 1]),
           pltpu.make_async_copy(ws2, g2b.at[pl.ds(4 * FF, FF)], esem.at[4, 2])]

    for c in range(8):
        qcp(c).start()
    for t in range(4):
        kcp(t).start()
        vcp(t).start()
    for c in range(8):
        ocp(c).start()
    scp[0].start()
    scp[1].start()

    mscr[...] = jnp.zeros((128, 128), F32)
    mscr[0:8, 0:16] = topk_ref[...].astype(F32)
    for i, part in enumerate(_split3(gates_ref[...])):
        mscr[8 + 8 * i:16 + 8 * i, 0:16] = part.astype(F32)
    mall[z, y, x, k] = mscr[...].T[0:16].astype(BF)
    a = _rms(x_ref[...], ln1_ref[...].reshape(1, D))

    own = mall.at[z, y, x, k]
    m1 = [_rcopy(own, own, mgs.at[i], mgr.at[i], d) for i, d in enumerate(p.column())]
    col = mall.at[:, :, x, k]
    m2 = [_rcopy(col, col, mgs.at[7 + i], mgr.at[7 + i], d) for i, d in enumerate(p.row())]

    def qstep(c, _):
        @pl.when(c == 5)
        def _():
            pl.semaphore_wait(barrier, 10)
            for cp in m1:
                cp.start()
        qcp(c).wait()
        q = _dot(a, g1b[:, pl.ds(pl.multiple_of(c * 512, 512), 512)]).astype(BF).astype(F32)
        for j in range(4):
            qs[pl.ds(pl.multiple_of(c * 64 + j * 16, 16), 16), :] = q[:, j * 128:(j + 1) * 128]
        return 0
    lax.fori_loop(0, 8, qstep, 0)
    for e in range(3):
        wcp(e, 0).start()
        wcp(e, 1).start()

    col = lax.broadcasted_iota(I32, (64, 1024), 1)
    row = lax.broadcasted_iota(I32, (64, 1024), 0)
    pos = jnp.where((col % 4) == (row % 32) // 8, col // 4, 1 << 20)
    first = lax.broadcasted_iota(I32, (64, 1), 0) < 32
    nil = jnp.zeros((32, 128), BF)

    def astep(g, _):
        @pl.when(g == 2)
        def _():
            for cp in m1:
                cp.wait_recv()
            for cp in m2:
                cp.start()
        kcp(g).wait()
        vcp(g).wait()
        for j in range(2):
            t = g * 4 + 2 * j
            qa = qs[pl.ds(t, 32, stride=16), :].astype(BF)
            qb = qs[pl.ds(t + 1, 32, stride=16), :].astype(BF)
            q2 = jnp.concatenate([jnp.concatenate([qa, nil], axis=1), jnp.concatenate([nil, qb], axis=1)], axis=0)
            s = _dot_tt(q2, jnp.concatenate([kb[t], kb[t + 1]], axis=1))
            s = jnp.where(pos < jnp.where(first, lens_ref[t], lens_ref[t + 1]), s, -jnp.inf)
            m = jnp.max(s, axis=1, keepdims=True)
            e = jnp.exp((s - m) * 128.0 ** -0.5)
            pr = (e * (1.0 / jnp.sum(e, axis=1, keepdims=True))).astype(BF)
            o = _dot(pr, jnp.concatenate([vb[t], vb[t + 1]], axis=1))
            os_[pl.ds(t, 32, stride=16), :] = o[:32, :128]
            os_[pl.ds(t + 1, 32, stride=16), :] = o[32:, 128:]
        return 0
    lax.fori_loop(0, 4, astep, 0)

    base[...] = x_ref[...].astype(F32)

    def ostep(c, _):
        ocp(c).wait()
        oc = jnp.concatenate([os_[pl.ds(pl.multiple_of(c * 64 + j * 16, 16), 16), :] for j in range(4)], axis=1).astype(BF)
        base[...] += _dot(oc, g2b[pl.ds(pl.multiple_of(c * 512, 512), 512), :])
        return 0
    lax.fori_loop(0, 8, ostep, 0)
    h = base[...].astype(BF)
    u_ref[...] = _rms(h, ln2_ref[...].reshape(1, D))
    base[...] = h.astype(F32)

    zc = []
    for c in range(NC):
        zb[c, z] = u_ref[:, CW * c:CW * (c + 1)]
    for c in range(NC):
        blk = zb.at[c, z]
        cps = [_rcopy(blk, blk, ags.at[c, d - 1], agr.at[c, d - 1], p.zdev(d)) for d in (1, 2, 3)]
        for cp in cps:
            cp.start()
        zc.append(cps)
    scp[2].start()
    for e in range(4):
        wcp(e, 2).start()

    for cp in m2:
        cp.wait_recv()
    def flags():
        mt = mall[...].reshape(NT, MW).astype(F32).T[0:32]
        mt_ref[...] = mt
        tk = mt[0:8]
        rm = jnp.concatenate([jnp.max(jnp.where((tk >= 16.0 * r) & (tk < 16.0 * r + 16.0), 1.0, 0.0), axis=0, keepdims=True)
                              for r in range(8)], axis=0)
        gt = (lax.broadcasted_iota(I32, (NT, 128), 0) // 16) % 8
        gsel = (gt == lax.broadcasted_iota(I32, (NT, 128), 1)).astype(F32).astype(BF)
        cnt = _dot(rm.astype(BF), gsel)
        flag_ref[0] = jnp.max(cnt).astype(I32)

    flags()
    tk = mt_ref[0:8]
    gts = (mt_ref[8:16], mt_ref[16:24], mt_ref[24:32])
    blk1 = lax.broadcasted_iota(I32, (1, NT), 1) // 16
    ti = lax.broadcasted_iota(I32, (NT, NT), 0)
    tj = lax.broadcasted_iota(I32, (NT, NT), 1)
    earlier = ti < tj
    fc[...] = jnp.where(earlier & ((ti // 16) % 8 == (tj // 16) % 8), 1.0, 0.0).astype(BF)

    def rowmatch(r):
        lo = (r * 16).astype(F32)
        return jnp.max(jnp.where((tk >= lo) & (tk < lo + 16.0), 1.0, 0.0), axis=0, keepdims=True)
    rm = jnp.concatenate([rowmatch(iy), rowmatch(z * 2 + (1 - y)), jnp.zeros((6, NT), F32)], axis=0)
    rb = _dot(rm.astype(BF), fc[...])
    rb = rb - win_ref[0].astype(F32) * capc
    ridx = jnp.where((rm > 0.5) & (rb > -0.5) & (rb < capc - 0.5), rb, -1.0)
    gidx = ((blk1 % 2) * 2 + (blk1 // 2) % 2) * 2 + (blk1 // 4) % 2
    mine = gidx == (k * 2 + x) * 2 + y
    sj = lax.broadcasted_iota(I32, (NT, 64), 1)
    st = lax.broadcasted_iota(I32, (NT, 64), 0)
    sel = (st == (sj // 16) * 128 + y * 64 + ix * 16 + sj % 16).astype(F32).astype(BF)

    def mylist(n):
        ci = lax.broadcasted_iota(I32, (n, NT), 0).astype(F32)
        own = jnp.concatenate([(ci == jnp.where(mine, ridx[i:i + 1], -1.0)).astype(F32) for i in range(2)], axis=0)
        return _dot(own.astype(BF), sel).astype(BF)
    emat = mylist(cap)
    ematc = mylist(capc) if capc != cap else emat

    yc = []
    for c in range(NC):
        for cp in zc[c]:
            cp.wait_recv()
        lst = _dot(emat, zb[c].reshape(64, CW)).astype(BF)
        yb[c] = lst[cap:]
        cp = _rcopy(yb.at[c], uc.at[c, k, x, y], ags.at[c, 3], agr.at[c, 3], p.ydev)
        cp.start()
        yc.append(cp)
        uc[c, k, x, y] = lst[:cap]

    scp[0].wait()
    scp[1].wait()
    u = u_ref[...]
    g = _dot(u, g1b[:, 6 * FF:7 * FF])
    v = _dot(u, g1b[:, 7 * FF:8 * FF])
    zs = (jax.nn.silu(g) * v).astype(BF)
    for i in range(2):
        wcp(3, i).start()

    xc = []
    for c in range(NC):
        yc[c].wait_recv()
        cp = _rcopy(uc.at[c, k, x], uc.at[c, k, x], ags.at[c, 4], agr.at[c, 4], p.xdev)
        cp.start()
        xc.append(cp)

    scp[2].wait()
    full = base[...] + _dot(zs, g2b[4 * FF:5 * FF, :]).astype(BF).astype(F32)
    base[...] = jnp.where(win_ref[0] == 0, full, 0.0)

    fc[...] = jnp.where(earlier & (ti // 16 == tj // 16), 1.0, 0.0).astype(BF)
    ms, gs = [], []
    for e in range(4):
        eq = tk == (dev * 4 + e).astype(F32)
        ms.append(jnp.sum(jnp.where(eq, 1.0, 0.0), axis=0, keepdims=True))
        gs.append([jnp.sum(jnp.where(eq, gg, 0.0), axis=0, keepdims=True) for gg in gts])
    mstack = jnp.concatenate(ms + [jnp.zeros((4, NT), F32)], axis=0)
    before = _dot(mstack.astype(BF), fc[...])
    slot = jnp.where((mstack > 0.5) & (before < CAPE - 0.5), (blk1 * CAPE).astype(F32) + before, -1.0)
    def allists(n):
        cidx = jnp.where(ridx[0:1] > -0.5, (gidx * n).astype(F32) + ridx[0:1], -1.0)
        return (lax.broadcasted_iota(I32, (8 * n, NT), 0).astype(F32) == cidx).astype(F32).astype(BF)
    cmat = allists(cap)
    cmatc = allists(capc) if capc != cap else cmat
    si = lax.broadcasted_iota(I32, (128, NT), 0).astype(F32)
    for e in range(4):
        hit = si == slot[e:e + 1]
        pm[128 * e:128 * (e + 1), :] = _dot_tt(hit.astype(F32).astype(BF), cmat).astype(BF)
        for m in range(3):
            gp = jnp.where(hit, gs[e][m], 0.0).astype(BF)
            gm[m, :, 128 * e:128 * (e + 1)] = _dot_tt(cmatc, gp).astype(BF)

    kc = []
    for c in range(NC):
        xc[c].wait_recv()
        cp = _rcopy(uc.at[c, k], uc.at[c, k], ags.at[c, 5], agr.at[c, 5], p.kdev)
        cp.start()
        kc.append(cp)
    for c in range(NC):
        kc[c].wait_recv()
        xe[:, :, c * CW:(c + 1) * CW] = _dot(pm[...], uc[c].reshape(8 * cap, CW)).astype(BF).reshape(4, 128, CW)

    def ffn(e, _):
        wcp(e, 0).wait()
        g = _dot(xe[e], g1b[:, col13(e, 0)])
        wcp(e, 1).wait()
        v = _dot(xe[e], g1b[:, col13(e, 1)])
        zz[e] = (jax.nn.silu(g) * v).astype(BF)
        return 0
    lax.fori_loop(0, 4, ffn, 0)
    for e in range(4):
        wcp(e, 2).wait()

    ca, cx, cy, cz = {}, {}, {}, {}

    def stage0(c):
        for e in range(4):
            fc[128 * e:128 * (e + 1), :] = _dot(zz[e], g2b[FF * e:FF * (e + 1), c * CX:(c + 1) * CX]).astype(BF)
        f = fc[...]
        o = _dot(gm[0], f) + _dot(gm[1], f) + _dot(gm[2], f)
        ps[c] = o.reshape(2, 2, 2, capc, CX)
        ca[c] = _rcopy(ps.at[c, 1 - k], ra.at[c], cbs.at[c, 0], cbr.at[c, 0], p.kdev)
        ca[c].start()

    def stage1(c):
        ca[c].wait_recv()
        ps[c, k] = ps[c, k] + ra[c]
        cx[c] = _rcopy(ps.at[c, k, 1 - x], rx.at[c], cbs.at[c, 1], cbr.at[c, 1], p.xdev)
        cx[c].start()

    def stage2(c):
        cx[c].wait_recv()
        ps[c, k, x] = ps[c, k, x] + rx[c]
        cy[c] = _rcopy(ps.at[c, k, x, 1 - y], ry.at[c], cbs.at[c, 2], cbr.at[c, 2], p.ydev)
        cy[c].start()

    def stage3(c):
        cy[c].wait_recv()
        data = jnp.concatenate([ps[c, k, x, y], ry[c]], axis=0)
        a, b, d = _split3(data)
        dn = _dot_00(ematc, a) + _dot_00(ematc, b) + _dot_00(ematc, d)
        dz_buf[c] = dn.reshape(4, 16, CX)
        cz[c] = [_rcopy(dz_buf.at[c, (z + d) % 4], rz.at[c, d - 1], cbs.at[c, 2 + d], cbr.at[c, 2 + d], p.zdev(d))
                 for d in (1, 2, 3)]
        for cp in cz[c]:
            cp.start()

    def stage4(c):
        for cp in cz[c]:
            cp.wait_recv()
        o = base[:, c * CX:(c + 1) * CX] + dz_buf[c, z] + rz[c, 0] + rz[c, 1] + rz[c, 2]
        out_ref[:, c * CX:(c + 1) * CX] = o

    stages = (stage0, stage1, stage2, stage3, stage4)
    for step in range(CC + 4):
        for s, fn in enumerate(stages):
            c = step - s
            if 0 <= c < CC:
                fn(c)
    for c in range(NC):
        for cp in zc[c] + [yc[c], xc[c], kc[c]]:
            cp.wait_send()
    for cp in m1 + m2:
        cp.wait_send()
    for c in range(CC):
        for cp in [ca[c], cx[c], cy[c]] + cz[c]:
            cp.wait_send()


def _layer(cap, capc, win, x, topk, gates, lens, ln1, ln2, *big):
    vm = pl.BlockSpec(memory_space=pltpu.VMEM)
    sm = pl.BlockSpec(memory_space=pltpu.SMEM)
    hb = pl.BlockSpec(memory_space=pl.ANY)
    dma = pltpu.SemaphoreType.DMA
    scratch = [
        pltpu.VMEM((D, 8 * FF), BF), pltpu.VMEM((4096, D), BF),
        pltpu.VMEM((16, 1024, 128), BF), pltpu.VMEM((16, 1024, 128), BF),
        pltpu.VMEM((512, 128), F32), pltpu.VMEM((512, 128), F32), pltpu.VMEM((4, 2, 2, 2, 16, MW), BF),
        pltpu.VMEM((128, 128), F32), pltpu.VMEM((32, NT), F32), pltpu.VMEM((16, D), BF),
        pltpu.VMEM((NC, 4, 16, CW), BF), pltpu.VMEM((NC, cap, CW), BF), pltpu.VMEM((NC, 2, 2, 2, cap, CW), BF),
        pltpu.VMEM((4, 128, D), BF), pltpu.VMEM((4, 128, FF), BF), pltpu.VMEM((512, 512), BF),
        pltpu.VMEM((3, 8 * capc, 512), BF), pltpu.VMEM((512, 8 * cap), BF),
        pltpu.VMEM((CC, 2, 2, 2, capc, CX), F32), pltpu.VMEM((CC, 2, 2, capc, CX), F32),
        pltpu.VMEM((CC, 2, capc, CX), F32), pltpu.VMEM((CC, capc, CX), F32),
        pltpu.VMEM((CC, 4, 16, CX), F32), pltpu.VMEM((CC, 3, 16, CX), F32), pltpu.VMEM((16, D), F32),
        dma((8,)), dma((8,)), dma((4,)), dma((4,)), dma((5, 3)), dma((10,)), dma((10,)),
        dma((NC, 6)), dma((NC, 6)), dma((CC, 6)), dma((CC, 6)),
    ]
    return pl.pallas_call(
        functools.partial(_layer_kernel, cap, capc),
        out_shape=(jax.ShapeDtypeStruct((16, D), F32), jax.ShapeDtypeStruct((1,), I32)),
        in_specs=[sm, vm, vm, vm, sm, vm, vm] + [hb] * 10,
        out_specs=(vm, sm),
        scratch_shapes=scratch,
        name='layer',
        compiler_params=pltpu.CompilerParams(collective_id=1, has_side_effects=True, vmem_limit_bytes=67_043_328),
    )(jnp.full((1,), win, I32), x, topk, gates, lens, ln1, ln2, *big)


CAPD = 32
CAPC = 24


def solution(mesh):
    rows = P(('ey', 'ex'))
    rep = P()

    def local(x, kv_k, kv_v, lens, topk_idx, gates, ln1, ln2, wq, wo, ws1, ws3, ws2, w1, w3, w2):
        args = (x, topk_idx.T, gates.T, lens, ln1, ln2, wq, wo, kv_k.reshape(16, 1024, 128), kv_v.reshape(16, 1024, 128),
                ws1, ws3, ws2, w1, w3, w2)
        acc, most = _layer(CAPD, CAPC, 0, *args)

        def more(acc, args):
            for win in range(1, -(-64 // CAPC)):
                acc += _layer(CAPD, CAPC, win, *args)[0]
            return acc
        return lax.cond(most[0] > CAPC, more, lambda acc, _: acc, acc, args).astype(BF)

    return jax.shard_map(
        local, mesh=mesh,
        in_specs=(rows, rows, rows, rows, rows, rows, rep, rep, rep, rep, rep, rep, rep, rows, rows, rows),
        out_specs=rows, check_vma=False)
```

time: 84 us -> 72.6 us (0.86); the launches traced: 83.6 us -> 71.2 us
  Pallas kernels: 75.3 us -> 68.8 us
  local copies, waits for them, and re-layouts: 6 us -> 0 us
    pallas_call x2 -> x1, Pallas kernels: 75.3 us -> 68.8 us  [_layer(): pl.pallas_call(functools.partial(_layer_kernel, cap, capc), out_shape=(ja...]
    broadcast_in_dim x3 -> x0, local copies, waits for them, and re-layouts: 2.58 us -> none  [the longest x1 1.29 us: local(): ln1[None]]
    unnamed x2 -> x0, local copies, waits for them, and re-layouts: 1.39 us -> none
    slice x1 -> x0, local copies, waits for them, and re-layouts: 1.2 us -> none  [local(): cnt[0, 0] > CAP + 0.5]
    convert_element_type x1, other arithmetic: 0.69 us -> 1.54 us  [local(): lax.cond(most[0] > CAPC, more, lambda acc, _: acc, acc, args).astype(BF)]
where the time goes in v3:
time: 72.6 us; the launch traced here: 71.2 us
  Pallas kernels  68.8 us (95%)
  other arithmetic  1.54 us (2%)
    pallas_call x1, Pallas kernels, _layer(): pl.pallas_call(functools.partial(_layer_kernel, cap, capc), out_shape=(ja...  68.8 us
    convert_element_type x1, other arithmetic, local(): lax.cond(most[0] > CAPC, more, lambda acc, _: acc, acc, args).astype(BF)  1.54 us

profile of v3, /device:TPU:0, one launch (start us, length us, event | category | flops | bytes accessed | tf_op | source)
XLA Modules:
  0.0 71.2 jit_solution(17967029168676808534)
XLA Ops:
  0.0 68.8 %layer.5 = (f32[16,2048]{1,0:T(8,128)}, s32[1]{0:T(128)}) custom-call(s32[1]{0:T(128)} %constant.3.clone.1.win_ref, bf16[16,2048]{1,0:T(8,128)(2,1)} %x_ref.1, s32[8,16]{1,0:T(8,128)} %bitcast.9, f32[8,16]{1,0:T(8,128)} %bitcast.11, s32[16]{0:T(128)} %lens_ref.1, bf16[2048]{0:T(1024)(128)(2,1)} %ln1_ref.1, bf16[2048]{0:T(1024)(128)(2,1)} %ln2_ref.1, ...), custom_call_target="tpu_custom_call" | custom-call | tf_op jit(solution)/shard_map/layer/pallas_call | solution.py:406
  69.5 0.2 conditional.5
  69.7 1.5 %convert_element_type.17 = bf16[16,2048]{1,0:T(8,128)(2,1)} convert(f32[16,2048]{1,0:T(8,128)} %get-tuple-element.74) | non-fusion elementwise | flops 32768 | bytes 196608 | tf_op jit(solution)/shard_map/convert_element_type | solution.py:434

commit v4 on v3

--- a/solution.py
+++ b/solution.py
@@ -83,14 +83,18 @@
         return [(self.iy, (self.ix + d) % 4) for d in range(1, 4)]
 
 
-def _layer_kernel(cap, capc, win_ref, x_ref, topk_ref, gates_ref, lens_ref, ln1_ref, ln2_ref,
+def _layer_kernel(cap, capc, win_ref, lens_ref, x_hbm, topk_hbm, gates_hbm, ln1_hbm, ln2_hbm,
                   wq, wo, kk, vv, ws1, ws3, ws2, w1, w3, w2, out_ref, flag_ref,
-                  g1b, g2b, kb, vb, qs, os_, mall, mscr, mt_ref, u_ref,
+                  x_ref, topk_ref, gates_ref, ln1_ref, ln2_ref, g1b, g2b, kb, vb, qs, os_, mall, mscr, mt_ref, u_ref,
                   zb, yb, uc, xe, zz, fc, gm, pm, ps, ra, rx, ry, dz_buf, rz, base,
-                  qsem, osem, ksem, vsem, esem, mgs, mgr, ags, agr, cbs, cbr):
+                  isem, qsem, osem, ksem, vsem, esem, mgs, mgr, ags, agr, cbs, cbr):
     p = _Pos()
     iy, ix, z, y, x, k = p.iy, p.ix, p.z, p.y, p.x, p.k
     dev = iy * 4 + ix
+    small = [pltpu.make_async_copy(s, d, isem.at[i]) for i, (s, d) in enumerate((
+        (x_hbm, x_ref), (topk_hbm, topk_ref), (gates_hbm, gates_ref), (ln1_hbm, ln1_ref), (ln2_hbm, ln2_ref)))]
+    for cp in small:
+        cp.start()
     barrier = p.greet()
 
     def qcp(c):
@@ -128,6 +132,8 @@
     scp[0].start()
     scp[1].start()
 
+    for cp in small:
+        cp.wait()
     mscr[...] = jnp.zeros((128, 128), F32)
     mscr[0:8, 0:16] = topk_ref[...].astype(F32)
     for i, part in enumerate(_split3(gates_ref[...])):
@@ -254,36 +260,41 @@
     emat = mylist(cap)
     ematc = mylist(capc) if capc != cap else emat
 
-    yc = []
-    for c in range(NC):
+    yc, xc, kc = {}, {}, {}
+
+    def ystep(c):
         for cp in zc[c]:
             cp.wait_recv()
         lst = _dot(emat, zb[c].reshape(64, CW)).astype(BF)
         yb[c] = lst[cap:]
-        cp = _rcopy(yb.at[c], uc.at[c, k, x, y], ags.at[c, 3], agr.at[c, 3], p.ydev)
-        cp.start()
-        yc.append(cp)
+        yc[c] = _rcopy(yb.at[c], uc.at[c, k, x, y], ags.at[c, 3], agr.at[c, 3], p.ydev)
+        yc[c].start()
         uc[c, k, x, y] = lst[:cap]
 
+    def xstep(c):
+        yc[c].wait_recv()
+        xc[c] = _rcopy(uc.at[c, k, x], uc.at[c, k, x], ags.at[c, 4], agr.at[c, 4], p.xdev)
+        xc[c].start()
+
+    def kstep(c):
+        xc[c].wait_recv()
+        kc[c] = _rcopy(uc.at[c, k], uc.at[c, k], ags.at[c, 5], agr.at[c, 5], p.kdev)
+        kc[c].start()
+
+    for c in range(NC):
+        ystep(c)
+    xstep(0)
+
     scp[0].wait()
-    scp[1].wait()
     u = u_ref[...]
     g = _dot(u, g1b[:, 6 * FF:7 * FF])
+    xstep(1)
+    scp[1].wait()
     v = _dot(u, g1b[:, 7 * FF:8 * FF])
     zs = (jax.nn.silu(g) * v).astype(BF)
     for i in range(2):
         wcp(3, i).start()
-
-    xc = []
-    for c in range(NC):
-        yc[c].wait_recv()
-        cp = _rcopy(uc.at[c, k, x], uc.at[c, k, x], ags.at[c, 4], agr.at[c, 4], p.xdev)
-        cp.start()
-        xc.append(cp)
-
-    scp[2].wait()
-    full = base[...] + _dot(zs, g2b[4 * FF:5 * FF, :]).astype(BF).astype(F32)
-    base[...] = jnp.where(win_ref[0] == 0, full, 0.0)
+    xstep(2)
 
     fc[...] = jnp.where(earlier & (ti // 16 == tj // 16), 1.0, 0.0).astype(BF)
     ms, gs = [], []
@@ -300,19 +311,20 @@
     cmat = allists(cap)
     cmatc = allists(capc) if capc != cap else cmat
     si = lax.broadcasted_iota(I32, (128, NT), 0).astype(F32)
+    xstep(3)
     for e in range(4):
+        if e > 1:
+            kstep(e - 2)
         hit = si == slot[e:e + 1]
         pm[128 * e:128 * (e + 1), :] = _dot_tt(hit.astype(F32).astype(BF), cmat).astype(BF)
         for m in range(3):
             gp = jnp.where(hit, gs[e][m], 0.0).astype(BF)
             gm[m, :, 128 * e:128 * (e + 1)] = _dot_tt(cmatc, gp).astype(BF)
-
-    kc = []
-    for c in range(NC):
-        xc[c].wait_recv()
-        cp = _rcopy(uc.at[c, k], uc.at[c, k], ags.at[c, 5], agr.at[c, 5], p.kdev)
-        cp.start()
-        kc.append(cp)
+    kstep(2)
+    scp[2].wait()
+    full = base[...] + _dot(zs, g2b[4 * FF:5 * FF, :]).astype(BF).astype(F32)
+    base[...] = jnp.where(win_ref[0] == 0, full, 0.0)
+    kstep(3)
     for c in range(NC):
         kc[c].wait_recv()
         xe[:, :, c * CW:(c + 1) * CW] = _dot(pm[...], uc[c].reshape(8 * cap, CW)).astype(BF).reshape(4, 128, CW)
@@ -332,8 +344,8 @@
 
     def stage0(c):
         for e in range(4):
-            fc[128 * e:128 * (e + 1), :] = _dot(zz[e], g2b[FF * e:FF * (e + 1), c * CX:(c + 1) * CX]).astype(BF)
-        f = fc[...]
+            fc[128 * e:128 * (e + 1), :CX] = _dot(zz[e], g2b[FF * e:FF * (e + 1), c * CX:(c + 1) * CX]).astype(BF)
+        f = fc[:, :CX]
         o = _dot(gm[0], f) + _dot(gm[1], f) + _dot(gm[2], f)
         ps[c] = o.reshape(2, 2, 2, capc, CX)
         ca[c] = _rcopy(ps.at[c, 1 - k], ra.at[c], cbs.at[c, 0], cbr.at[c, 0], p.kdev)
@@ -369,11 +381,9 @@
         out_ref[:, c * CX:(c + 1) * CX] = o
 
     stages = (stage0, stage1, stage2, stage3, stage4)
-    for step in range(CC + 4):
-        for s, fn in enumerate(stages):
-            c = step - s
-            if 0 <= c < CC:
-                fn(c)
+    due = [0, 2, 6.6, 10.8, 17]
+    for _, n, c in sorted((due[n] + c * (2.7 if n else 1.5), n, c) for n in range(5) for c in range(CC)):
+        stages[n](c)
     for c in range(NC):
         for cp in zc[c] + [yc[c], xc[c], kc[c]]:
             cp.wait_send()
@@ -390,6 +400,7 @@
     hb = pl.BlockSpec(memory_space=pl.ANY)
     dma = pltpu.SemaphoreType.DMA
     scratch = [
+        pltpu.VMEM((16, D), BF), pltpu.VMEM((8, 16), I32), pltpu.VMEM((8, 16), F32), pltpu.VMEM((D,), BF), pltpu.VMEM((D,), BF),
         pltpu.VMEM((D, 8 * FF), BF), pltpu.VMEM((4096, D), BF),
         pltpu.VMEM((16, 1024, 128), BF), pltpu.VMEM((16, 1024, 128), BF),
         pltpu.VMEM((512, 128), F32), pltpu.VMEM((512, 128), F32), pltpu.VMEM((4, 2, 2, 2, 16, MW), BF),
@@ -400,18 +411,18 @@
         pltpu.VMEM((CC, 2, 2, 2, capc, CX), F32), pltpu.VMEM((CC, 2, 2, capc, CX), F32),
         pltpu.VMEM((CC, 2, capc, CX), F32), pltpu.VMEM((CC, capc, CX), F32),
         pltpu.VMEM((CC, 4, 16, CX), F32), pltpu.VMEM((CC, 3, 16, CX), F32), pltpu.VMEM((16, D), F32),
-        dma((8,)), dma((8,)), dma((4,)), dma((4,)), dma((5, 3)), dma((10,)), dma((10,)),
+        dma((5,)), dma((8,)), dma((8,)), dma((4,)), dma((4,)), dma((5, 3)), dma((10,)), dma((10,)),
         dma((NC, 6)), dma((NC, 6)), dma((CC, 6)), dma((CC, 6)),
     ]
     return pl.pallas_call(
         functools.partial(_layer_kernel, cap, capc),
         out_shape=(jax.ShapeDtypeStruct((16, D), F32), jax.ShapeDtypeStruct((1,), I32)),
-        in_specs=[sm, vm, vm, vm, sm, vm, vm] + [hb] * 10,
+        in_specs=[sm, sm] + [hb] * 15,
         out_specs=(vm, sm),
         scratch_shapes=scratch,
         name='layer',
         compiler_params=pltpu.CompilerParams(collective_id=1, has_side_effects=True, vmem_limit_bytes=67_043_328),
-    )(jnp.full((1,), win, I32), x, topk, gates, lens, ln1, ln2, *big)
+    )(jnp.full((1,), win, I32), lens, x, topk, gates, ln1, ln2, *big)
 
 
 CAPD = 32

time: 72.6 us -> 70.1 us (0.966); the launches traced: 71.2 us -> 69.9 us
  Pallas kernels: 68.8 us -> 67.5 us
    pallas_call x1, Pallas kernels: 68.8 us -> 67.5 us  [_layer(): pl.pallas_call(functools.partial(_layer_kernel, cap, capc), out_shape=(ja...]
where the time goes in v4:
time: 70.1 us; the launch traced here: 69.9 us
  Pallas kernels  67.5 us (96%)
  other arithmetic  1.54 us (2%)
    pallas_call x1, Pallas kernels, _layer(): pl.pallas_call(functools.partial(_layer_kernel, cap, capc), out_shape=(ja...  67.5 us
    convert_element_type x1, other arithmetic, local(): lax.cond(most[0] > CAPC, more, lambda acc, _: acc, acc, args).astype(BF)  1.54 us

profile of v4, /device:TPU:0, one launch (start us, length us, event | category | flops | bytes accessed | tf_op | source)
XLA Modules:
  0.0 69.9 jit_solution(3624895610226032395)
XLA Ops:
  0.0 67.5 %layer.5 = (f32[16,2048]{1,0:T(8,128)}, s32[1]{0:T(128)}) custom-call(s32[1]{0:T(128)} %constant.3.clone.1.win_ref, s32[16]{0:T(128)} %lens_ref.1, bf16[16,2048]{1,0:T(8,128)(2,1)} %x_hbm.1, s32[8,16]{1,0:T(8,128)} %bitcast.9, f32[8,16]{1,0:T(8,128)} %bitcast.11, bf16[2048]{0:T(1024)(128)(2,1)} %ln1_hbm.1, bf16[2048]{0:T(1024)(128)(2,1)} %ln2_hbm.1, ...), custom_call_target="tpu_custom_call" | custom-call | tf_op jit(solution)/shard_map/layer/pallas_call | solution.py:417
  68.1 0.2 conditional.5
  68.4 1.5 %convert_element_type.17 = bf16[16,2048]{1,0:T(8,128)(2,1)} convert(f32[16,2048]{1,0:T(8,128)} %get-tuple-element.74) | non-fusion elementwise | flops 32768 | bytes 196608 | tf_op jit(solution)/shard_map/convert_element_type | solution.py:445

commit v5 on v4

--- a/solution.py
+++ b/solution.py
@@ -210,7 +210,7 @@
         zb[c, z] = u_ref[:, CW * c:CW * (c + 1)]
     for c in range(NC):
         blk = zb.at[c, z]
-        cps = [_rcopy(blk, blk, ags.at[c, d - 1], agr.at[c, d - 1], p.zdev(d)) for d in (1, 2, 3)]
+        cps = [_rcopy(blk, blk, ags.at[c, d - 1], agr.at[c, d - 1], p.zdev(d)) for d in (2, 1, 3)]
         for cp in cps:
             cp.start()
         zc.append(cps)
@@ -370,7 +370,7 @@
         dn = _dot_00(ematc, a) + _dot_00(ematc, b) + _dot_00(ematc, d)
         dz_buf[c] = dn.reshape(4, 16, CX)
         cz[c] = [_rcopy(dz_buf.at[c, (z + d) % 4], rz.at[c, d - 1], cbs.at[c, 2 + d], cbr.at[c, 2 + d], p.zdev(d))
-                 for d in (1, 2, 3)]
+                 for d in (2, 1, 3)]
         for cp in cz[c]:
             cp.start()
 

time: 70.1 us -> 70.4 us (level)
  no operation moved by 1% of the time
where the time goes in v5:
time: 70.4 us; the launch traced here: 70.3 us
  Pallas kernels  67.9 us (96%)
  other arithmetic  1.54 us (2%)
    pallas_call x1, Pallas kernels, _layer(): pl.pallas_call(functools.partial(_layer_kernel, cap, capc), out_shape=(ja...  67.9 us
    convert_element_type x1, other arithmetic, local(): lax.cond(most[0] > CAPC, more, lambda acc, _: acc, acc, args).astype(BF)  1.54 us

profile of v5, /device:TPU:0, one launch (start us, length us, event | category | flops | bytes accessed | tf_op | source)
XLA Modules:
  0.0 70.3 jit_solution(9094576007073994867)
XLA Ops:
  0.0 67.9 %layer.5 = (f32[16,2048]{1,0:T(8,128)}, s32[1]{0:T(128)}) custom-call(s32[1]{0:T(128)} %constant.3.clone.1.win_ref, s32[16]{0:T(128)} %lens_ref.1, bf16[16,2048]{1,0:T(8,128)(2,1)} %x_hbm.1, s32[8,16]{1,0:T(8,128)} %bitcast.9, f32[8,16]{1,0:T(8,128)} %bitcast.11, bf16[2048]{0:T(1024)(128)(2,1)} %ln1_hbm.1, bf16[2048]{0:T(1024)(128)(2,1)} %ln2_hbm.1, ...), custom_call_target="tpu_custom_call" | custom-call | tf_op jit(solution)/shard_map/layer/pallas_call | solution.py:417
  68.5 0.2 conditional.5
  68.7 1.5 %convert_element_type.17 = bf16[16,2048]{1,0:T(8,128)(2,1)} convert(f32[16,2048]{1,0:T(8,128)} %get-tuple-element.74) | non-fusion elementwise | flops 32768 | bytes 196608 | tf_op jit(solution)/shard_map/convert_element_type | solution.py:445
